TPU v7x, 512 devices: a whole 4x8x8 slice. The times are simulated.
512 devices in a mesh: lon: 32 (over y, x_hi, core), lat: 16 (over x_lo, z).
Axes of the slice: x: 4 (x_hi: 2, x_lo: 2; x = x_hi * 2 + x_lo), y: 8, z: 8, core: 2. Of those that a mesh axis runs over, the one named last changes fastest.
Arguments:
- latent: bfloat16 [4, 256, 512, 320], P(None, 'lat', 'lon'), may hold values from -28 to 28, as said below
- norm1_gain: float32 [320], replicated, may hold values from 0.1 to 1.9
- norm1_shift: float32 [320], replicated, may hold values from -3 to 3
- conv1_weight: bfloat16 [3, 3, 320, 320], replicated, may hold values from -0.109375 to 0.109375
- conv1_bias: float32 [320], replicated, may hold values from -3 to 3
- emb_shift: float32 [4, 320], replicated, may hold values from -4 to 4
- norm2_gain: float32 [320], replicated, may hold values from 0.1 to 1.9
- norm2_shift: float32 [320], replicated, may hold values from -3 to 3
- conv2_weight: bfloat16 [3, 3, 320, 320], replicated, may hold values from -0.109375 to 0.109375
- conv2_bias: float32 [320], replicated, may hold values from -3 to 3
Outputs:
- block_out: bfloat16 [4, 256, 512, 320], P(None, 'lat', 'lon')
Inputs may be any that keep to these rules, and one draw needn't show every extreme that they name: `latent`: Real-valued activations.
All inputs are finite; a program needn't handle non-finite values.
Results may differ from a plain program's by a relative error of at most 0.007.
Values may be sent and summed in bfloat16 or wider, within the bound.
A program may use at most 64 MiB of HBM per device.

v0:
```python
import functools

import jax
import jax.numpy as jnp
from jax import lax
from jax.sharding import Mesh
from jax.sharding import PartitionSpec as P

GROUPS = 32
LON_LAT = ("lon_0", "lon_1", "lon_2", "lat_0", "lat_1")
LON = ("lon_0", "lon_1", "lon_2")
LAT = ("lat_0", "lat_1")


def over_axes(array, axes):
    return functools.reduce(lax.psum, axes, array)


def padded_2(array, sides, width, wrap):
    for axis, dim in sides:
        devices, length = (lax.axis_size(axis), array.shape[dim])
        up = [(i, (i + 1) % devices) for i in range(devices if wrap else devices - 1)]
        down = [(j, i) for i, j in up]
        last = lax.slice_in_dim(array, length - width, length, axis=dim)
        leading = lax.slice_in_dim(array, 0, width, axis=dim)
        before = lax.ppermute(last, axis, up)
        after = lax.ppermute(leading, axis, down)
        array = jnp.concatenate([before, array, after], axis=dim)
    return array


def from_behind(array, axis, by):
    devices = lax.axis_size(axis)
    return lax.ppermute(array, axis, [(i, (i + by) % devices) for i in range(devices)])


def group_stats(field, cell_count):
    frame_count = field.shape[0]
    grouped = field.reshape(frame_count, -1, GROUPS, field.shape[3] // GROUPS)
    summed, squares = (
        over_axes(jnp.sum(grouped, axis=(1, 3)), LON_LAT),
        over_axes(jnp.sum(grouped * grouped, axis=(1, 3)), LON_LAT),
    )
    average = summed / cell_count
    variance = squares / cell_count - average * average
    return (average, lax.rsqrt(variance + 1e-05))


def activate(field, average, inverse, norm_gain, norm_shift):
    per_group = field.shape[3] // GROUPS
    per_mean = jnp.repeat(average, per_group, axis=1)[:, None, None, :]
    per_inverse = jnp.repeat(inverse, per_group, axis=1)[:, None, None, :]
    normed = (field - per_mean) * per_inverse * norm_gain + norm_shift
    return jax.nn.silu(normed).astype(jnp.bfloat16)


def sphere_pad(field):
    side_padded = padded_2(field, ((LON, 2),), 1, True)
    both_padded = padded_2(side_padded, ((LAT, 1),), 1, False)
    north_row, south_row = from_behind(
        (side_padded[:, 0], side_padded[:, -1]), LON, lax.axis_size(LON) // 2
    )
    lat_index = lax.axis_index(LAT)
    first_row = jnp.where(lat_index == 0, north_row, both_padded[:, 0])
    final_row = jnp.where(lat_index == lax.axis_size(LAT) - 1, south_row, both_padded[:, -1])
    return jnp.concatenate([first_row[:, None], both_padded[:, 1:-1], final_row[:, None]], axis=1)


def padded_input(source, cell_count, norm_gain, norm_shift):
    source_f = source.astype(jnp.float32)
    average, inverse = group_stats(source_f, cell_count)
    padded = sphere_pad(source)
    return activate(padded.astype(jnp.float32), average, inverse, norm_gain, norm_shift)


def convolve(padded, weight):
    return lax.conv_general_dilated(
        padded,
        weight,
        (1, 1),
        "VALID",
        dimension_numbers=("NHWC", "HWIO", "NHWC"),
        preferred_element_type=jnp.float32,
    )


def on_device(
    latent,
    norm1_gain,
    norm1_shift,
    conv1_weight,
    conv1_bias,
    emb_shift,
    norm2_gain,
    norm2_shift,
    conv2_weight,
    conv2_bias,
):
    per_group = latent.shape[3] // GROUPS
    cell_count = (
        latent.shape[1] * latent.shape[2] * lax.axis_size(LAT) * lax.axis_size(LON) * per_group
    )
    first_padded = padded_input(latent, cell_count, norm1_gain, norm1_shift)
    hidden = convolve(first_padded, conv1_weight) + conv1_bias + emb_shift[:, None, None, :]
    hidden = hidden.astype(jnp.bfloat16)
    second_padded = padded_input(hidden, cell_count, norm2_gain, norm2_shift)
    branch = convolve(second_padded, conv2_weight) + conv2_bias
    return (latent.astype(jnp.float32) + branch).astype(jnp.bfloat16)


def solution(mesh):
    torus = Mesh(mesh.devices.reshape(8, 2, 2, 2, 8), ("lon_0", "lon_1", "lon_2", "lat_0", "lat_1"))
    return jax.shard_map(
        on_device,
        mesh=torus,
        in_specs=(P(None, LAT, LON, None), P(), P(), P(), P(), P(), P(), P(), P(), P()),
        out_specs=P(None, LAT, LON, None),
        check_vma=False,
    )
```

profile of v0, /device:TPU:8, one launch (start us, length us, event | category | flops | bytes accessed | tf_op | source)
XLA Modules:
  0.0 195.7 jit_solution(6362441920269768431)
XLA Ops:
  0.0 1.4 fusion.27
  1.5 1.9 collective-permute-start
  3.5 6.0 %collective-permute-start.1 = (bf16[4,16,1,320]{3,0,2,1:T(4,128)(2,1)S(1)}, bf16[4,16,1,320]{3,0,2,1:T(4,128)(2,1)S(1)}, u32[]{:S(2)}, u32[]{:S(2)}) collective-permute-start(bf16[4,16,1,320]{3,0,2,1:T(4,128)(2,1)S(1)} %copy.99), channel_id=1, source_target_pairs={{16,0},{32,16},{48,32},{64,48},{80,64},{96,80},{112,96},{128,112},... | collective-permute-start | bytes 122888 | tf_op jit(solution)/shard_map/ppermute | solution.py:27
  9.5 1.4 convert_reduce_fusion
  11.4 21.1 %all-reduce.3 = (f32[4,32]{1,0:T(4,128)S(1)}, f32[4,32]{1,0:T(4,128)S(1)}) all-reduce(f32[4,32]{1,0:T(4,128)S(1)} %reduce_sum.54, f32[4,32]{1,0:T(4,128)S(1)} %reduce_sum.51), channel_id=1, replica_groups=mesh['lon_0'=8,'lon_1'=2,'lon_2'=2,'lat_0'=2,'lat_1'=8] {'lon_0'}, use_global_device_ids=true, to_apply=%region_9.0 | all-reduce | flops 256 | bytes 2048 | tf_op jit(solution)/shard_map/psum | solution.py:16
  32.5 6.4 %all-reduce.9 = (f32[4,32]{1,0:T(4,128)S(1)}, f32[4,32]{1,0:T(4,128)S(1)}) all-reduce(f32[4,32]{1,0:T(4,128)S(1)} %get-tuple-element.13, f32[4,32]{1,0:T(4,128)S(1)} %get-tuple-element.14), channel_id=1, replica_groups=mesh['lon_0'=8,'lon_1'=2,'lon_2'=2,'lat_0'=2,'lat_1'=8] {'lon_1'}, use_global_device_ids=true, to_apply=%region_10.0 | all-reduce | flops 256 | bytes 2048 | tf_op jit(solution)/shard_map/psum | solution.py:16
  38.9 2.4 %all-reduce.7 = (f32[4,32]{1,0:T(4,128)S(1)}, f32[4,32]{1,0:T(4,128)S(1)}) all-reduce(f32[4,32]{1,0:T(4,128)S(1)} %get-tuple-element.25, f32[4,32]{1,0:T(4,128)S(1)} %get-tuple-element.26), channel_id=1, replica_groups=mesh['lon_0'=8,'lon_1'=2,'lon_2'=2,'lat_0'=2,'lat_1'=8] {'lon_2'}, use_global_device_ids=true, to_apply=%region_11.0 | all-reduce | flops 256 | bytes 2048 | tf_op jit(solution)/shard_map/psum | solution.py:16
  41.4 4.9 %all-reduce.5 = (f32[4,32]{1,0:T(4,128)S(1)}, f32[4,32]{1,0:T(4,128)S(1)}) all-reduce(f32[4,32]{1,0:T(4,128)S(1)} %get-tuple-element.21, f32[4,32]{1,0:T(4,128)S(1)} %get-tuple-element.22), channel_id=1, replica_groups=mesh['lon_0'=8,'lon_1'=2,'lon_2'=2,'lat_0'=2,'lat_1'=8] {'lat_0'}, use_global_device_ids=true, to_apply=%region_12.13 | all-reduce | flops 256 | bytes 2048 | tf_op jit(solution)/shard_map/psum | solution.py:16
  46.3 18.9 %all-reduce.1 = (f32[4,32]{1,0:T(4,128)S(1)}, f32[4,32]{1,0:T(4,128)S(1)}) all-reduce(f32[4,32]{1,0:T(4,128)S(1)} %get-tuple-element.17, f32[4,32]{1,0:T(4,128)S(1)} %get-tuple-element.18), channel_id=1, replica_groups=mesh['lon_0'=8,'lon_1'=2,'lon_2'=2,'lat_0'=2,'lat_1'=8] {'lat_1'}, use_global_device_ids=true, to_apply=%region_13.14 | all-reduce | flops 256 | bytes 2048 | tf_op jit(solution)/shard_map/psum | solution.py:16
  67.0 1.3 collective-permute-start.3
  68.3 6.7 %collective-permute-start.2 = (bf16[4,18,320]{2,0,1:T(4,128)(2,1)S(1)}, bf16[4,18,320]{2,0,1:T(4,128)(2,1)S(1)}, u32[]{:S(2)}, u32[]{:S(2)}) collective-permute-start(bf16[4,18,320]{2,0,1:T(4,128)(2,1)S(1)} %get-tuple-element.30), channel_id=1, source_target_pairs={{0,256},{16,272},{32,288},{48,304},{64,320},{80,336},{96,352},{112... | collective-permute-start | bytes 138248 | tf_op jit(solution)/shard_map/ppermute | solution.py:34
  75.4 3.1 %collective-permute-start.4 = (bf16[4,18,320]{2,0,1:T(4,128)(2,1)S(1)}, bf16[4,18,320]{2,0,1:T(4,128)(2,1)S(1)}, u32[]{:S(2)}, u32[]{:S(2)}) collective-permute-start(bf16[4,18,320]{2,0,1:T(4,128)(2,1)S(1)} %get-tuple-element.31), channel_id=1, source_target_pairs={{0,256},{16,272},{32,288},{48,304},{64,320},{80,336},{96,352},{112... | collective-permute-start | bytes 138248 | tf_op jit(solution)/shard_map/ppermute | solution.py:34
  78.4 1.5 collective-permute-start.5
  80.0 5.6 %collective-permute-done.4 = bf16[4,18,320]{2,0,1:T(4,128)(2,1)S(1)} collective-permute-done((bf16[4,18,320]{2,0,1:T(4,128)(2,1)S(1)}, bf16[4,18,320]{2,0,1:T(4,128)(2,1)S(1)}, u32[]{:S(2)}, u32[]{:S(2)}) %collective-permute-start.4) | collective-permute-done | bytes 46112 | tf_op jit(solution)/shard_map/ppermute | solution.py:34
  85.7 2.7 %fusion.19 = bf16[18,4,18,320]{3,1,2,0:T(4,128)(2,1)S(1)} fusion(bf16[4,1,18,320]{3,0,2,1:T(4,128)(2,1)S(1)} %fusion.23, bf16[4,16,18,320]{3,0,2,1:T(4,128)(2,1)} %copy-done.3, bf16[4,1,18,320]{3,0,2,1:T(4,128)(2,1)S(1)} %fusion.24, f32[320]{0:T(512)S(1)} %copy-done.5, f32[320]{0:T(512)S(1)} %copy-done.6, f32[4,320]{1,0:T(4,128)S(1)} %mul.64, ...), kind=kLoop, calls=%fused_computation.26 | loop fusion | flops 4976640 | bytes 1671680 | tf_op jit(solution)/shard_map/convert_element_type | solution.py:54
  90.9 5.6 %convert_multiply_fusion.1 = (f32[16,32,3,320]{3,1,2,0:T(8,128)S(1)}, bf16[16,32,3,320]{3,1,2,0:T(8,128)(2,1)S(1)}) fusion(f32[16,32,3,320]{3,0,2,1:T(8,128)S(1)} %bitcast.73, f32[320]{0:T(512)S(1)} %copy-done.10, bf16[3,3,320,320]{3,2,1,0:T(8,128)(2,1)S(1)} %copy-done, bf16[18,4,8,5,320]{4,1,3,2,0:T(4,128)(2,1)S(1)} %fusion.3, pred[32,3]{0,1:T(4,128)(4,1)S(1)} %copy-done.12), kind=kOutput, calls=%fused_computation.29 | convolution fusion | flops 2834104320 | bytes 8602976 | tf_op jit(solution)/shard_map/conv_general_dilated | solution.py:77
  97.3 1.4 copy.73
  100.4 1.9 collective-permute-start.6
  102.4 6.0 %collective-permute-start.7 = (bf16[4,16,1,320]{3,0,2,1:T(4,128)(2,1)S(1)}, bf16[4,16,1,320]{3,0,2,1:T(4,128)(2,1)S(1)}, u32[]{:S(2)}, u32[]{:S(2)}) collective-permute-start(bf16[4,16,1,320]{3,0,2,1:T(4,128)(2,1)S(1)} %get-tuple-element.34), channel_id=1, source_target_pairs={{16,0},{32,16},{48,32},{64,48},{80,64},{96,80},{112,96},{128,112},... | collective-permute-start | bytes 122888 | tf_op jit(solution)/shard_map/ppermute | solution.py:27
  109.0 15.4 %all-reduce.2 = (f32[4,32]{1,0:T(4,128)S(1)}, f32[4,32]{1,0:T(4,128)S(1)}) all-reduce(f32[4,32]{1,0:T(4,128)S(1)} %reduce_sum.75, f32[4,32]{1,0:T(4,128)S(1)} %reduce_sum.72), channel_id=1, replica_groups=mesh['lon_0'=8,'lon_1'=2,'lon_2'=2,'lat_0'=2,'lat_1'=8] {'lon_0'}, use_global_device_ids=true, to_apply=%region_23.24 | all-reduce | flops 256 | bytes 2048 | tf_op jit(solution)/shard_map/psum | solution.py:16
  124.4 6.4 %all-reduce.8 = (f32[4,32]{1,0:T(4,128)S(1)}, f32[4,32]{1,0:T(4,128)S(1)}) all-reduce(f32[4,32]{1,0:T(4,128)S(1)} %get-tuple-element.11, f32[4,32]{1,0:T(4,128)S(1)} %get-tuple-element.12), channel_id=1, replica_groups=mesh['lon_0'=8,'lon_1'=2,'lon_2'=2,'lat_0'=2,'lat_1'=8] {'lon_1'}, use_global_device_ids=true, to_apply=%region_24.25 | all-reduce | flops 256 | bytes 2048 | tf_op jit(solution)/shard_map/psum | solution.py:16
  130.8 2.4 %all-reduce.6 = (f32[4,32]{1,0:T(4,128)S(1)}, f32[4,32]{1,0:T(4,128)S(1)}) all-reduce(f32[4,32]{1,0:T(4,128)S(1)} %get-tuple-element.23, f32[4,32]{1,0:T(4,128)S(1)} %get-tuple-element.24), channel_id=1, replica_groups=mesh['lon_0'=8,'lon_1'=2,'lon_2'=2,'lat_0'=2,'lat_1'=8] {'lon_2'}, use_global_device_ids=true, to_apply=%region_25.26 | all-reduce | flops 256 | bytes 2048 | tf_op jit(solution)/shard_map/psum | solution.py:16
  133.3 6.8 %all-reduce.4 = (f32[4,32]{1,0:T(4,128)S(1)}, f32[4,32]{1,0:T(4,128)S(1)}) all-reduce(f32[4,32]{1,0:T(4,128)S(1)} %get-tuple-element.19, f32[4,32]{1,0:T(4,128)S(1)} %get-tuple-element.20), channel_id=1, replica_groups=mesh['lon_0'=8,'lon_1'=2,'lon_2'=2,'lat_0'=2,'lat_1'=8] {'lat_0'}, use_global_device_ids=true, to_apply=%region_26.27 | all-reduce | flops 256 | bytes 2048 | tf_op jit(solution)/shard_map/psum | solution.py:16
  140.1 19.2 %all-reduce = (f32[4,32]{1,0:T(4,128)S(1)}, f32[4,32]{1,0:T(4,128)S(1)}) all-reduce(f32[4,32]{1,0:T(4,128)S(1)} %get-tuple-element.15, f32[4,32]{1,0:T(4,128)S(1)} %get-tuple-element.16), channel_id=1, replica_groups=mesh['lon_0'=8,'lon_1'=2,'lon_2'=2,'lat_0'=2,'lat_1'=8] {'lat_1'}, use_global_device_ids=true, to_apply=%region_27.28 | all-reduce | flops 256 | bytes 2048 | tf_op jit(solution)/shard_map/psum | solution.py:16
  160.1 5.5 %collective-permute-start.10 = (bf16[4,18,320]{2,0,1:T(4,128)(2,1)S(1)}, bf16[4,18,320]{2,0,1:T(4,128)(2,1)S(1)}, u32[]{:S(2)}, u32[]{:S(2)}) collective-permute-start(bf16[4,18,320]{2,0,1:T(4,128)(2,1)S(1)} %bitcast.74), channel_id=1, source_target_pairs={{0,256},{16,272},{32,288},{48,304},{64,320},{80,336},{96,352},{112... | collective-permute-start | bytes 138248 | tf_op jit(solution)/shard_map/ppermute | solution.py:34
  165.6 1.5 collective-permute-start.11
  167.6 4.5 %collective-permute-start.9 = (bf16[4,1,18,320]{3,0,2,1:T(4,128)(2,1)S(1)}, bf16[4,1,18,320]{3,0,2,1:T(4,128)(2,1)S(1)}, u32[]{:S(2)}, u32[]{:S(2)}) collective-permute-start(bf16[4,1,18,320]{3,0,2,1:T(4,128)(2,1)S(1)} %get-tuple-element.28), channel_id=1, source_target_pairs={{0,1},{1,2},{2,3},{3,4},{4,5},{5,6},{6,7},{7,8},{8,9},{9,10},{10,1... | collective-permute-start | bytes 138248 | tf_op jit(solution)/shard_map/ppermute | solution.py:26
  172.1 4.2 %collective-permute-start.8 = (bf16[4,18,320]{2,0,1:T(4,128)(2,1)S(1)}, bf16[4,18,320]{2,0,1:T(4,128)(2,1)S(1)}, u32[]{:S(2)}, u32[]{:S(2)}) collective-permute-start(bf16[4,18,320]{2,0,1:T(4,128)(2,1)S(1)} %bitcast.75), channel_id=1, source_target_pairs={{0,256},{16,272},{32,288},{48,304},{64,320},{80,336},{96,352},{112... | collective-permute-start | bytes 138248 | tf_op jit(solution)/shard_map/ppermute | solution.py:34
  176.5 5.9 %collective-permute-done.8 = bf16[4,18,320]{2,0,1:T(4,128)(2,1)S(1)} collective-permute-done((bf16[4,18,320]{2,0,1:T(4,128)(2,1)S(1)}, bf16[4,18,320]{2,0,1:T(4,128)(2,1)S(1)}, u32[]{:S(2)}, u32[]{:S(2)}) %collective-permute-start.8) | collective-permute-done | bytes 46112 | tf_op jit(solution)/shard_map/ppermute | solution.py:34
  182.4 3.1 %fusion.20 = bf16[18,4,18,320]{3,1,2,0:T(4,128)(2,1)S(1)} fusion(bf16[4,1,18,320]{3,0,2,1:T(4,128)(2,1)S(1)} %fusion.21, bf16[4,16,1,320]{3,0,2,1:T(4,128)(2,1)S(1)} %collective-permute-done.7, bf16[4,16,16,320]{3,0,2,1:T(4,128)(2,1)} %bitcast.68, bf16[4,16,1,320]{3,0,2,1:T(4,128)(2,1)S(1)} %collective-permute-done.6, ...), kind=kLoop, calls=%fused_computation.27 | loop fusion | flops 5806080 | bytes 1671680 | tf_op jit(solution)/shard_map/convert_element_type | solution.py:54
  188.0 5.0 %select_add_fusion = f32[16,32,3,320]{3,1,2,0:T(8,128)S(1)} fusion(bf16[3,3,320,320]{3,2,1,0:T(8,128)(2,1)S(1)} %copy-done.9, bf16[18,4,8,5,320]{4,1,3,2,0:T(4,128)(2,1)S(1)} %fusion.4, f32[320]{0:T(512)S(1)} %copy-done.11, pred[32,3]{0,1:T(4,128)(4,1)S(1)} %copy-done.12), kind=kOutput, calls=%fused_computation.8 | convolution fusion | flops 2832138240 | bytes 5653856 | tf_op jit(solution)/shard_map/conv_general_dilated | solution.py:77
  193.0 1.4 copy.75
  (81 shorter events, 13.3 us)
Async XLA Ops:
  0.0 90.4 %copy-start = (bf16[3,3,320,320]{3,2,1,0:T(8,128)(2,1)S(1)}, bf16[3,3,320,320]{3,2,1,0:T(8,128)(2,1)}, u32[]{:S(2)}) copy-start(bf16[3,3,320,320]{3,2,1,0:T(8,128)(2,1)} %param.13) | copy-start | bytes 5529604
  0.0 65.2 %copy-start.1 = (bf16[4,16,16,320]{3,2,1,0:T(8,128)(2,1)S(1)}, bf16[4,16,16,320]{3,2,1,0:T(8,128)(2,1)}, u32[]{:S(2)}) copy-start(bf16[4,16,16,320]{3,2,1,0:T(8,128)(2,1)} %param.10) | copy-start | bytes 1966084
  0.0 85.6 %copy-start.5 = (f32[320]{0:T(512)S(1)}, f32[320]{0:T(512)}, u32[]{:S(2)}) copy-start(f32[320]{0:T(512)} %param.12) | copy-start | bytes 3844
  0.0 85.6 %copy-start.6 = (f32[320]{0:T(512)S(1)}, f32[320]{0:T(512)}, u32[]{:S(2)}) copy-start(f32[320]{0:T(512)} %param.11) | copy-start | bytes 3844
  1.5 63.7 %collective-permute-start = (bf16[4,16,1,320]{3,0,2,1:T(4,128)(2,1)S(1)}, bf16[4,16,1,320]{3,0,2,1:T(4,128)(2,1)S(1)}, u32[]{:S(2)}, u32[]{:S(2)}) collective-permute-start(bf16[4,16,1,320]{3,0,2,1:T(4,128)(2,1)S(1)} %copy.98), channel_id=1, source_target_pairs={{0,16},{16,32},{32,48},{48,64},{64,80},{80,96},{96,112},{112,128},... | collective-permute-start | bytes 122888 | tf_op jit(solution)/shard_map/ppermute | solution.py:26
  3.5 62.5 %collective-permute-start.1 = (bf16[4,16,1,320]{3,0,2,1:T(4,128)(2,1)S(1)}, bf16[4,16,1,320]{3,0,2,1:T(4,128)(2,1)S(1)}, u32[]{:S(2)}, u32[]{:S(2)}) collective-permute-start(bf16[4,16,1,320]{3,0,2,1:T(4,128)(2,1)S(1)} %copy.99), channel_id=1, source_target_pairs={{16,0},{32,16},{48,32},{64,48},{80,64},{96,80},{112,96},{128,112},... | collective-permute-start | bytes 122888 | tf_op jit(solution)/shard_map/ppermute | solution.py:27
  66.0 0.9 copy-start.3
  67.0 13.0 %collective-permute-start.3 = (bf16[4,1,18,320]{3,0,2,1:T(4,128)(2,1)S(1)}, bf16[4,1,18,320]{3,0,2,1:T(4,128)(2,1)S(1)}, u32[]{:S(2)}, u32[]{:S(2)}) collective-permute-start(bf16[4,1,18,320]{3,0,2,1:T(4,128)(2,1)S(1)} %get-tuple-element.29), channel_id=1, source_target_pairs={{0,1},{1,2},{2,3},{3,4},{4,5},{5,6},{6,7},{7,8},{8,9},{9,10},{10,1... | collective-permute-start | bytes 138248 | tf_op jit(solution)/shard_map/ppermute | solution.py:26
  68.3 11.7 %collective-permute-start.2 = (bf16[4,18,320]{2,0,1:T(4,128)(2,1)S(1)}, bf16[4,18,320]{2,0,1:T(4,128)(2,1)S(1)}, u32[]{:S(2)}, u32[]{:S(2)}) collective-permute-start(bf16[4,18,320]{2,0,1:T(4,128)(2,1)S(1)} %get-tuple-element.30), channel_id=1, source_target_pairs={{0,256},{16,272},{32,288},{48,304},{64,320},{80,336},{96,352},{112... | collective-permute-start | bytes 138248 | tf_op jit(solution)/shard_map/ppermute | solution.py:34
  75.4 10.2 %collective-permute-start.4 = (bf16[4,18,320]{2,0,1:T(4,128)(2,1)S(1)}, bf16[4,18,320]{2,0,1:T(4,128)(2,1)S(1)}, u32[]{:S(2)}, u32[]{:S(2)}) collective-permute-start(bf16[4,18,320]{2,0,1:T(4,128)(2,1)S(1)} %get-tuple-element.31), channel_id=1, source_target_pairs={{0,256},{16,272},{32,288},{48,304},{64,320},{80,336},{96,352},{112... | collective-permute-start | bytes 138248 | tf_op jit(solution)/shard_map/ppermute | solution.py:34
  78.4 7.2 %collective-permute-start.5 = (bf16[4,1,18,320]{3,0,2,1:T(4,128)(2,1)S(1)}, bf16[4,1,18,320]{3,0,2,1:T(4,128)(2,1)S(1)}, u32[]{:S(2)}, u32[]{:S(2)}) collective-permute-start(bf16[4,1,18,320]{3,0,2,1:T(4,128)(2,1)S(1)} %get-tuple-element.32), channel_id=1, source_target_pairs={{1,0},{2,1},{3,2},{4,3},{5,4},{6,5},{7,6},{8,7},{9,8},{10,9},{11,1... | collective-permute-start | bytes 138248 | tf_op jit(solution)/shard_map/ppermute | solution.py:27
  89.1 1.1 copy-start.4
  90.2 0.7 copy-start.10
  90.2 0.7 copy-start.12
  99.5 0.9 copy-start.2
  99.5 82.9 %copy-start.7 = (f32[320]{0:T(512)S(1)}, f32[320]{0:T(512)}, u32[]{:S(2)}) copy-start(f32[320]{0:T(512)} %param.17) | copy-start | bytes 3844
  99.5 82.9 %copy-start.8 = (f32[320]{0:T(512)S(1)}, f32[320]{0:T(512)}, u32[]{:S(2)}) copy-start(f32[320]{0:T(512)} %param.16) | copy-start | bytes 3844
  100.4 58.8 %collective-permute-start.6 = (bf16[4,16,1,320]{3,0,2,1:T(4,128)(2,1)S(1)}, bf16[4,16,1,320]{3,0,2,1:T(4,128)(2,1)S(1)}, u32[]{:S(2)}, u32[]{:S(2)}) collective-permute-start(bf16[4,16,1,320]{3,0,2,1:T(4,128)(2,1)S(1)} %get-tuple-element.33), channel_id=1, source_target_pairs={{0,16},{16,32},{32,48},{48,64},{64,80},{80,96},{96,112},{112,128},... | collective-permute-start | bytes 122888 | tf_op jit(solution)/shard_map/ppermute | solution.py:26
  102.4 56.9 %collective-permute-start.7 = (bf16[4,16,1,320]{3,0,2,1:T(4,128)(2,1)S(1)}, bf16[4,16,1,320]{3,0,2,1:T(4,128)(2,1)S(1)}, u32[]{:S(2)}, u32[]{:S(2)}) collective-permute-start(bf16[4,16,1,320]{3,0,2,1:T(4,128)(2,1)S(1)} %get-tuple-element.34), channel_id=1, source_target_pairs={{16,0},{32,16},{48,32},{64,48},{80,64},{96,80},{112,96},{128,112},... | collective-permute-start | bytes 122888 | tf_op jit(solution)/shard_map/ppermute | solution.py:27
  160.1 16.3 %collective-permute-start.10 = (bf16[4,18,320]{2,0,1:T(4,128)(2,1)S(1)}, bf16[4,18,320]{2,0,1:T(4,128)(2,1)S(1)}, u32[]{:S(2)}, u32[]{:S(2)}) collective-permute-start(bf16[4,18,320]{2,0,1:T(4,128)(2,1)S(1)} %bitcast.74), channel_id=1, source_target_pairs={{0,256},{16,272},{32,288},{48,304},{64,320},{80,336},{96,352},{112... | collective-permute-start | bytes 138248 | tf_op jit(solution)/shard_map/ppermute | solution.py:34
  165.6 10.8 %collective-permute-start.11 = (bf16[4,1,18,320]{3,0,2,1:T(4,128)(2,1)S(1)}, bf16[4,1,18,320]{3,0,2,1:T(4,128)(2,1)S(1)}, u32[]{:S(2)}, u32[]{:S(2)}) collective-permute-start(bf16[4,1,18,320]{3,0,2,1:T(4,128)(2,1)S(1)} %get-tuple-element.27), channel_id=1, source_target_pairs={{1,0},{2,1},{3,2},{4,3},{5,4},{6,5},{7,6},{8,7},{9,8},{10,9},{11,1... | collective-permute-start | bytes 138248 | tf_op jit(solution)/shard_map/ppermute | solution.py:27
  167.6 14.8 %collective-permute-start.9 = (bf16[4,1,18,320]{3,0,2,1:T(4,128)(2,1)S(1)}, bf16[4,1,18,320]{3,0,2,1:T(4,128)(2,1)S(1)}, u32[]{:S(2)}, u32[]{:S(2)}) collective-permute-start(bf16[4,1,18,320]{3,0,2,1:T(4,128)(2,1)S(1)} %get-tuple-element.28), channel_id=1, source_target_pairs={{0,1},{1,2},{2,3},{3,4},{4,5},{5,6},{6,7},{7,8},{8,9},{9,10},{10,1... | collective-permute-start | bytes 138248 | tf_op jit(solution)/shard_map/ppermute | solution.py:26
  172.1 10.2 %collective-permute-start.8 = (bf16[4,18,320]{2,0,1:T(4,128)(2,1)S(1)}, bf16[4,18,320]{2,0,1:T(4,128)(2,1)S(1)}, u32[]{:S(2)}, u32[]{:S(2)}) collective-permute-start(bf16[4,18,320]{2,0,1:T(4,128)(2,1)S(1)} %bitcast.75), channel_id=1, source_target_pairs={{0,256},{16,272},{32,288},{48,304},{64,320},{80,336},{96,352},{112... | collective-permute-start | bytes 138248 | tf_op jit(solution)/shard_map/ppermute | solution.py:34
  186.4 1.6 copy-start.9
  186.4 1.6 copy-start.11
where the time goes:
time: 196 us
  blocking collectives  104 us (53%)
  starting transfers between devices  44.3 us (23%)
  local copies, waits for them, and re-layouts  13.3 us (7%)
  waiting for transfers between devices  11.6 us (6%)
  other arithmetic  11.3 us (6%)
  matrix products  10.6 us (5%)
    psum x10, blocking collectives, over_axes(): return functools.reduce(lax.psum, axes, array)  104 us
    ppermute x4, starting transfers between devices, from_behind(): lax.ppermute(array, axis, [(i, (i + by) % devices) for i in range(devices)])  19.5 us
    ppermute x4, starting transfers between devices, padded_2(): after = lax.ppermute(leading, axis, down)  15.1 us
    ppermute x4, waiting for transfers between devices, from_behind(): lax.ppermute(array, axis, [(i, (i + by) % devices) for i in range(devices)])  11.5 us
    conv_general_dilated x2, matrix products, convolve(): lax.conv_general_dilated(padded, weight, (1, 1), 'VALID', dimension_numbe...  10.6 us
    ppermute x4, starting transfers between devices, padded_2(): before = lax.ppermute(last, axis, up)  9.68 us
    convert_element_type x2, other arithmetic, activate(): return jax.nn.silu(normed).astype(jnp.bfloat16)  5.81 us
    unnamed x31, local copies, waits for them, and re-layouts  4.26 us
  transfers between devices with their start and end apart: 12, of which 2 were waited for; matrix products, arithmetic and copies ran while one was open for 2% of the time, Pallas kernels for 0%

commit v1 on v0

v1 whole, which is shorter than its diff:
```python
import functools

import jax
import jax.numpy as jnp
from jax import lax
from jax.experimental import pallas as pl
from jax.experimental.pallas import tpu as pltpu
from jax.sharding import PartitionSpec as P

GROUPS = 32
F = 4
T = 16
C = 320
KP = 384
F32 = jnp.float32
BF16 = jnp.bfloat16
MESH = pl.DeviceIdType.MESH


def kernel(
    n_lon,
    n_lat,
    x_hbm,
    g1_ref,
    s1_ref,
    w1_hbm,
    b1_ref,
    emb_ref,
    g2_ref,
    s2_ref,
    w2_hbm,
    b2_ref,
    o_ref,
    xv,
    hid,
    w1v,
    w2v,
    cols,
    stat,
    coef,
    msg,
    sums,
    rowbuf,
    colbuf,
    corbuf,
    colsend,
    corsend,
    x_sem,
    w_sem,
    ar_send,
    ar_recv,
    row_send,
    row_recv,
    col_send,
    col_recv,
    cor_send,
    cor_recv,
):
    n_y, n_z, half = n_lon // 4, n_lat // 2, n_lon // 2
    lon, lat = lax.axis_index("lon"), lax.axis_index("lat")
    y, x_hi, core = lon // 4, (lon // 2) % 2, lon % 2
    x_lo, z = lat // n_z, lat % n_z

    x_in = [pltpu.make_async_copy(x_hbm.at[f], xv.at[f], x_sem.at[f]) for f in range(F)]
    for cp in x_in:
        cp.start()
    w_in = []
    for k, (hbm, vm) in enumerate(((w1_hbm, w1v), (w2_hbm, w2v))):
        for a in range(3):
            for b in range(3):
                w_in.append(
                    pltpu.make_async_copy(
                        hbm.at[a, b], vm.at[a, pl.ds(b * KP, C)], w_sem.at[k, 3 * a + b]
                    )
                )
                w_in[-1].start()

    def flip(bit, on):
        return 1 - bit if on else bit

    stages = [[], [], []]
    for d in range(1, 8):
        h, c, l = flip(x_hi, d & 4), flip(core, d & 2), flip(x_lo, d & 1)
        stages[0].append((d, (y * 4 + h * 2 + c, l * n_z + z)))
    for d in range(1, n_y):
        stages[1].append((d, (((y + d) % n_y) * 4 + x_hi * 2 + core, lat)))
    for d in range(1, n_z):
        stages[2].append((d, (lon, x_lo * n_z + (z + d) % n_z)))

    at_pole = [(lat == 0).astype(jnp.int32), (lat == n_lat - 1).astype(jnp.int32)]
    row_lat = [lat - 1 + at_pole[0], lat + 1 - at_pole[1]]
    row_shift = [half * at_pole[0], half * at_pole[1]]
    row_side = [1 - at_pole[0], at_pole[1]]
    row_dev = [((lon + row_shift[v]) % n_lon, row_lat[v]) for v in range(2)]
    col_dev = [((lon + n_lon - 1) % n_lon, lat), ((lon + 1) % n_lon, lat)]
    cor_dev = [
        [((lon + row_shift[v] + n_lon + (2 * h - 1)) % n_lon, row_lat[v]) for h in range(2)]
        for v in range(2)
    ]

    barrier = pltpu.get_barrier_semaphore()
    greeted = [dev for stage in stages for _, dev in stage]
    greeted += row_dev + col_dev + cor_dev[0] + cor_dev[1]
    for dev in greeted:
        pl.semaphore_signal(barrier, inc=1, device_id=dev, device_id_type=MESH)

    for b in range(3):
        cols[:, :, pl.ds(b * KP + 256, 128)] = jnp.zeros((F, 18 * T, 128), BF16)
        for a in range(3):
            w1v[a, pl.ds(b * KP + C, KP - C), :] = jnp.zeros((KP - C, C), BF16)
            w2v[a, pl.ds(b * KP + C, KP - C), :] = jnp.zeros((KP - C, C), BF16)

    chan = lax.broadcasted_iota(jnp.int32, (C, 128), 0)
    group = lax.broadcasted_iota(jnp.int32, (C, 128), 1) % GROUPS
    per = C // GROUPS
    member = jnp.where((chan >= group * per) & (chan < group * per + per), 1.0, 0.0).astype(F32)
    row8 = lax.broadcasted_iota(jnp.int32, (8, 128), 0)
    lane8 = lax.broadcasted_iota(jnp.int32, (8, 128), 1)
    own_frame = (row8 % F) == (lane8 // GROUPS)

    def note_frame(f, v):
        flat = v.reshape(T * T, C)
        stat[pl.ds(f, 1), :] = jnp.sum(flat, axis=0, keepdims=True)
        stat[pl.ds(F + f, 1), :] = jnp.sum(flat * flat, axis=0, keepdims=True)
        for h, c in enumerate((0, T - 1)):
            column = v[:, c, :]
            colsend[h, f] = column.astype(BF16)
            for side, r in enumerate((0, T - 1)):
                corsend[side, h, pl.ds(f, 1), :] = column[r : r + 1, :]

    def exchange(p, src):
        sent = []
        for v, r in enumerate((0, T - 1)):
            sent.append(
                pltpu.make_async_remote_copy(
                    src_ref=src.at[:, r],
                    dst_ref=rowbuf.at[p, row_side[v]],
                    send_sem=row_send.at[p, v],
                    recv_sem=row_recv.at[p, row_side[v]],
                    device_id=row_dev[v],
                    device_id_type=MESH,
                )
            )
        for h in range(2):
            sent.append(
                pltpu.make_async_remote_copy(
                    src_ref=colsend.at[h],
                    dst_ref=colbuf.at[p, 1 - h],
                    send_sem=col_send.at[p, h],
                    recv_sem=col_recv.at[p, 1 - h],
                    device_id=col_dev[h],
                    device_id_type=MESH,
                )
            )
            for v in range(2):
                sent.append(
                    pltpu.make_async_remote_copy(
                        src_ref=corsend.at[v, h],
                        dst_ref=corbuf.at[p, row_side[v], 1 - h],
                        send_sem=cor_send.at[p, v, h],
                        recv_sem=cor_recv.at[p, row_side[v], 1 - h],
                        device_id=cor_dev[v][h],
                        device_id_type=MESH,
                    )
                )
        return sent

    def landed(p):
        for k in range(2):
            pltpu.make_async_copy(rowbuf.at[p, k], rowbuf.at[p, k], row_recv.at[p, k]).wait()
            pltpu.make_async_copy(colbuf.at[p, k], colbuf.at[p, k], col_recv.at[p, k]).wait()
            for h in range(2):
                pltpu.make_async_copy(
                    corbuf.at[p, k, h], corbuf.at[p, k, h], cor_recv.at[p, k, h]
                ).wait()

    def reduce_stats(p, between):
        per_group = jnp.dot(
            stat[...], member, precision=lax.Precision.HIGHEST, preferred_element_type=F32
        )
        picked = jnp.where(own_frame, per_group, 0.0)
        total = jnp.concatenate(
            [jnp.sum(picked[:F], axis=0, keepdims=True), jnp.sum(picked[F:], axis=0, keepdims=True)],
            axis=0,
        )
        sent = []
        for s, peers in enumerate(stages):
            msg[p, s] = total
            here = []
            for d, dev in peers:
                here.append(
                    pltpu.make_async_remote_copy(
                        src_ref=msg.at[p, s],
                        dst_ref=sums.at[p, s, d],
                        send_sem=ar_send.at[p, s, d],
                        recv_sem=ar_recv.at[p, s, d],
                        device_id=dev,
                        device_id_type=MESH,
                    )
                )
                here[-1].start()
            if s == 0:
                between()
            for cp in here:
                cp.wait_recv()
            for d, _ in peers:
                total = total + sums[p, s, d]
            sent += here
        for cp in sent:
            cp.wait_send()
        return total

    def coefficients(total, gain, shift):
        count = float(T * T * n_lon * n_lat * per)
        average = total[0:1] / count
        variance = total[1:2] / count - average * average
        inverse = lax.rsqrt(variance + 1e-05)
        both = jnp.concatenate(
            [jnp.broadcast_to(average, (F, 128)), jnp.broadcast_to(inverse, (F, 128))], axis=0
        )
        spread = lax.dot_general(
            jnp.where(own_frame, both, 0.0),
            member,
            (((1,), (1,)), ((), ())),
            precision=lax.Precision.HIGHEST,
            preferred_element_type=F32,
        )
        coef[0:8, :] = spread
        coef[8:9, :] = gain * 0.5
        coef[9:10, :] = shift * 0.5

    def convolve(p, f, src, wv):
        mean = coef[pl.ds(f, 1), :]
        scale = coef[pl.ds(F + f, 1), :] * coef[8:9, :]
        shift = coef[9:10, :]

        def act(v):
            lead = (1,) * (v.ndim - 2)
            m, k, s = (t.reshape(lead + (1, C)) for t in (mean, scale, shift))
            h = (v - m) * k + s
            return h + h * jnp.tanh(h)

        rows = jnp.concatenate([rowbuf[p, 0, f][None], src[f], rowbuf[p, 1, f][None]], axis=0)
        mid = act(rows.astype(F32))
        side = []
        for h in range(2):
            strip = jnp.concatenate(
                [
                    corbuf[p, 0, h, pl.ds(f, 1), :],
                    colbuf[p, h, f].astype(F32),
                    corbuf[p, 1, h, pl.ds(f, 1), :],
                ],
                axis=0,
            )
            side.append(act(strip)[:, None, :])
        west = jnp.concatenate([side[0], mid[:, : T - 1, :]], axis=1)
        east = jnp.concatenate([mid[:, 1:, :], side[1]], axis=1)
        for b, v in enumerate((west, mid, east)):
            cols[f, :, pl.ds(b * KP, C)] = v.astype(BF16).reshape(18 * T, C)
        acc = jnp.zeros((T * T, C), F32)
        for a in range(3):
            acc += jnp.dot(
                cols[f, pl.ds(a * T, T * T), :], wv[a], preferred_element_type=F32
            )
        return acc

    for f in range(F):
        x_in[f].wait()

    def first_notes(f, carry):
        note_frame(f, xv[f].astype(F32))
        return carry

    lax.fori_loop(0, F, first_notes, 0)
    pl.semaphore_wait(barrier, len(greeted))
    sent = exchange(0, xv)

    def start_all(copies):
        for cp in copies:
            cp.start()

    total = reduce_stats(0, lambda: start_all(sent))
    coefficients(total, g1_ref[...], s1_ref[...])
    landed(0)
    for cp in sent:
        cp.wait_send()
    for cp in w_in:
        cp.wait()

    def first_conv(f, carry):
        acc = convolve(0, f, xv, w1v)
        acc = acc + b1_ref[...] + emb_ref[pl.ds(f, 1), :]
        rounded = acc.astype(BF16).reshape(T, T, C)
        hid[f] = rounded
        note_frame(f, rounded.astype(F32))
        return carry

    lax.fori_loop(0, F, first_conv, 0)

    sent = exchange(1, hid)
    total = reduce_stats(1, lambda: start_all(sent))
    coefficients(total, g2_ref[...], s2_ref[...])
    landed(1)
    for cp in sent:
        cp.wait_send()

    def second_conv(f, carry):
        acc = convolve(1, f, hid, w2v)
        acc = acc + b2_ref[...] + xv[f].astype(F32).reshape(T * T, C)
        o_ref[f] = acc.astype(BF16).reshape(T, T, C)
        return carry

    lax.fori_loop(0, F, second_conv, 0)


def block(n_lon, n_lat, latent, g1, s1, w1, b1, emb, g2, s2, w2, b2):
    vm = pl.BlockSpec(memory_space=pltpu.VMEM)
    hbm = pl.BlockSpec(memory_space=pl.ANY)
    dma = pltpu.SemaphoreType.DMA
    row = lambda v: v.reshape(1, C)
    return pl.pallas_call(
        functools.partial(kernel, n_lon, n_lat),
        out_shape=jax.ShapeDtypeStruct((F, T, T, C), BF16),
        in_specs=[hbm, vm, vm, hbm, vm, vm, vm, vm, hbm, vm],
        out_specs=vm,
        scratch_shapes=[
            pltpu.VMEM((F, T, T, C), BF16),
            pltpu.VMEM((F, T, T, C), BF16),
            pltpu.VMEM((3, 3 * KP, C), BF16),
            pltpu.VMEM((3, 3 * KP, C), BF16),
            pltpu.VMEM((F, 18 * T, 3 * KP), BF16),
            pltpu.VMEM((8, C), F32),
            pltpu.VMEM((16, C), F32),
            pltpu.VMEM((2, 3, 2, 128), F32),
            pltpu.VMEM((2, 3, 8, 2, 128), F32),
            pltpu.VMEM((2, 2, F, T, C), BF16),
            pltpu.VMEM((2, 2, F, T, C), BF16),
            pltpu.VMEM((2, 2, 2, 8, C), F32),
            pltpu.VMEM((2, F, T, C), BF16),
            pltpu.VMEM((2, 2, 8, C), F32),
            dma((F,)),
            dma((2, 9)),
            dma((2, 3, 8)),
            dma((2, 3, 8)),
            dma((2, 2)),
            dma((2, 2)),
            dma((2, 2)),
            dma((2, 2)),
            dma((2, 2, 2)),
            dma((2, 2, 2)),
        ],
        compiler_params=pltpu.CompilerParams(collective_id=0, has_side_effects=True),
    )(latent, row(g1), row(s1), w1, row(b1), emb, row(g2), row(s2), w2, row(b2))


def solution(mesh):
    n_lon, n_lat = mesh.shape["lon"], mesh.shape["lat"]
    tile = P(None, "lat", "lon", None)
    return jax.shard_map(
        functools.partial(block, n_lon, n_lat),
        mesh=mesh,
        in_specs=(tile,) + (P(),) * 9,
        out_specs=tile,
        check_vma=False,
    )
```

time: 196 us -> 64 us (0.33)
  the two profiles are of different devices: /device:TPU:8 before, /device:TPU:1 now
where the time goes in v1:
time: 64 us; the launch traced here: 63.7 us
  Pallas kernels  54 us (84%)
  local copies, waits for them, and re-layouts  9.62 us (15%)
    pallas_call x1, Pallas kernels, block(): pl.pallas_call(functools.partial(kernel, n_lon, n_lat), out_shape=jax.Sha...  54 us
    reshape x6, local copies, waits for them, and re-layouts, block(): row = lambda v: v.reshape(1, C)  7.53 us
    unnamed x1, local copies, waits for them, and re-layouts  2.09 us

profile of v1, /device:TPU:1, one launch (start us, length us, event | category | flops | bytes accessed | tf_op | source)
XLA Modules:
  0.0 63.7 jit_solution(16436054782955168976)
XLA Ops:
  0.0 1.2 %reshape.18.g1_ref = f32[1,320]{1,0:T(1,128)} reshape(f32[320]{0:T(512)} %param.11) | data formatting | bytes 2560 | tf_op jit(solution)/shard_map/reshape | solution.py:320
  1.2 1.3 %reshape.19.s1_ref = f32[1,320]{1,0:T(1,128)} reshape(f32[320]{0:T(512)} %param.12) | data formatting | bytes 2560 | tf_op jit(solution)/shard_map/reshape | solution.py:320
  2.5 1.3 %reshape.20.b1_ref = f32[1,320]{1,0:T(1,128)} reshape(f32[320]{0:T(512)} %param.14) | data formatting | bytes 2560 | tf_op jit(solution)/shard_map/reshape | solution.py:320
  3.8 1.2 %reshape.21.g2_ref = f32[1,320]{1,0:T(1,128)} reshape(f32[320]{0:T(512)} %param.16) | data formatting | bytes 2560 | tf_op jit(solution)/shard_map/reshape | solution.py:320
  5.0 1.3 %reshape.22.s2_ref = f32[1,320]{1,0:T(1,128)} reshape(f32[320]{0:T(512)} %param.17) | data formatting | bytes 2560 | tf_op jit(solution)/shard_map/reshape | solution.py:320
  6.3 1.3 %reshape.23.b2_ref = f32[1,320]{1,0:T(1,128)} reshape(f32[320]{0:T(512)} %param.19) | data formatting | bytes 2560 | tf_op jit(solution)/shard_map/reshape | solution.py:320
  7.5 54.0 %shard_map.100 = bf16[4,16,16,320]{3,2,1,0:T(8,128)(2,1)} custom-call(bf16[4,16,16,320]{3,2,1,0:T(8,128)(2,1)} %x_hbm.1, f32[1,320]{1,0:T(1,128)} %reshape.18.g1_ref, f32[1,320]{1,0:T(1,128)} %reshape.19.s1_ref, bf16[3,3,320,320]{3,2,1,0:T(8,128)(2,1)} %w1_hbm.1, f32[1,320]{1,0:T(1,128)} %reshape.20.b1_ref, f32[4,320]{1,0:T(4,128)} %emb_ref.1, ...), custom_call_target="tpu_custom_call" | custom-call | tf_op jit(solution)/shard_map/pallas_call | solution.py:321
  61.6 2.1 %copy.12 = bf16[4,16,16,320]{3,2,1,0:T(8,128)(2,1)} copy(bf16[4,16,16,320]{3,2,1,0:T(8,128)(2,1)} %shard_map.100) | data formatting | bytes 1310720

commit v2 on v1

v2 whole, which is shorter than its diff:
```python
import functools

import jax
import jax.numpy as jnp
from jax import lax
from jax.experimental import pallas as pl
from jax.experimental.pallas import tpu as pltpu
from jax.sharding import PartitionSpec as P

GROUPS = 32
F = 4
T = 16
C = 320
LOW = 256
TAIL = C - LOW
K = 1024
F32 = jnp.float32
BF16 = jnp.bfloat16
MESH = pl.DeviceIdType.MESH


def kernel(
    n_lon,
    n_lat,
    x_hbm,
    g1_hbm,
    s1_hbm,
    w1_hbm,
    b1_hbm,
    emb_hbm,
    g2_hbm,
    s2_hbm,
    w2_hbm,
    b2_hbm,
    o_ref,
    xv,
    hid,
    wf,
    wt,
    cols,
    stat,
    coef,
    vecs,
    emb,
    msg,
    sums,
    halo,
    corner,
    colsend,
    corsend,
    x_sem,
    w_sem,
    v_sem,
    ar_send,
    ar_recv,
    halo_send,
    halo_recv,
    cor_send,
    cor_recv,
):
    n_y, n_z, half = n_lon // 4, n_lat // 2, n_lon // 2
    rem, div = lax.rem, lax.div
    lon, lat = lax.axis_index("lon"), lax.axis_index("lat")
    y, x_hi, core = div(lon, 4), rem(div(lon, 2), 2), rem(lon, 2)
    x_lo, z = div(lat, n_z), rem(lat, n_z)

    x_in = [pltpu.make_async_copy(x_hbm.at[f], xv.at[f], x_sem.at[f]) for f in range(F)]
    for cp in x_in:
        cp.start()

    def flip(bit, on):
        return 1 - bit if on else bit

    stages = [[], []]
    for d in range(1, 2 * n_y):
        to_y = rem(y + d // 2, n_y)
        stages[0].append((to_y * 4 + x_hi * 2 + flip(core, d % 2), lat))
    for d in range(1, 4 * n_z):
        to_z = rem(z + d // 4, n_z)
        to_lon = y * 4 + flip(x_hi, d & 1) * 2 + core
        stages[1].append((to_lon, flip(x_lo, d & 2) * n_z + to_z))

    at_pole = [(lat == 0).astype(jnp.int32), (lat == n_lat - 1).astype(jnp.int32)]
    row_lat = [lat - 1 + at_pole[0], lat + 1 - at_pole[1]]
    row_shift = [half * at_pole[0], half * at_pole[1]]
    row_side = [1 - at_pole[0], at_pole[1]]
    row_dev = [(rem(lon + row_shift[v], n_lon), row_lat[v]) for v in range(2)]
    col_dev = [(rem(lon + n_lon - 1, n_lon), lat), (rem(lon + 1, n_lon), lat)]
    cor_dev = [
        [(rem(lon + row_shift[v] + n_lon + (2 * h - 1), n_lon), row_lat[v]) for h in range(2)]
        for v in range(2)
    ]

    barrier = pltpu.get_barrier_semaphore()
    greeted = [dev for stage in stages for dev in stage]
    greeted += row_dev + col_dev + cor_dev[0] + cor_dev[1]
    for dev in greeted:
        pl.semaphore_signal(barrier, inc=1, device_id=dev, device_id_type=MESH)

    vec_in = [
        pltpu.make_async_copy(hbm, vecs.at[i], v_sem.at[i])
        for i, hbm in enumerate((g1_hbm, s1_hbm, b1_hbm, g2_hbm, s2_hbm, b2_hbm))
    ]
    vec_in.append(pltpu.make_async_copy(emb_hbm, emb, v_sem.at[6]))
    for cp in vec_in:
        cp.start()
    for k, hbm in enumerate((w1_hbm, w2_hbm)):
        for a in range(3):
            for b in range(3):
                pltpu.make_async_copy(
                    hbm.at[a, b, pl.ds(0, LOW)], wf.at[k, a, pl.ds(b * LOW, LOW)], w_sem.at[k]
                ).start()
                pltpu.make_async_copy(
                    hbm.at[a, b, pl.ds(LOW, TAIL)],
                    wf.at[k, a, pl.ds(3 * LOW + b * TAIL, TAIL)],
                    w_sem.at[k],
                ).start()

    per = C // GROUPS

    def member(shape, channel_dim):
        chan = lax.broadcasted_iota(jnp.int32, shape, channel_dim)
        group = lax.broadcasted_iota(jnp.int32, shape, 1 - channel_dim) & (GROUPS - 1)
        inside = (chan >= group * per) & (chan < group * per + per)
        return jnp.where(inside, 1.0, 0.0).astype(BF16)

    own_frame = (lax.broadcasted_iota(jnp.int32, (8, 128), 0) & (F - 1)) == (
        lax.broadcasted_iota(jnp.int32, (8, 128), 1) // GROUPS
    )

    def select(v, chosen):
        high = v.astype(BF16).astype(F32)
        middle = (v - high).astype(BF16).astype(F32)
        low = v - high - middle
        parts = jnp.concatenate([high, middle, low], axis=0).astype(BF16)
        out = jnp.dot(parts, chosen, preferred_element_type=F32)
        return out[0:8] + out[8:16] + out[16:24]

    def note_frame(f, v):
        flat = v.reshape(T * T, C)
        stat[pl.ds(f, 1), :] = jnp.sum(flat, axis=0, keepdims=True)
        stat[pl.ds(F + f, 1), :] = jnp.sum(flat * flat, axis=0, keepdims=True)
        for h, c in enumerate((0, T - 1)):
            column = v[:, c, :]
            colsend[h, f] = column.astype(BF16)
            for side, r in enumerate((0, T - 1)):
                corsend[side, h, pl.ds(f, 1), :] = column[r : r + 1, :]

    def remote(src, dst, send, recv, dev):
        pltpu.make_async_remote_copy(
            src_ref=src,
            dst_ref=dst,
            send_sem=send,
            recv_sem=recv,
            device_id=dev,
            device_id_type=MESH,
        ).start()

    def arrived(ref, sem):
        pltpu.make_async_copy(ref, ref, sem).wait()

    def exchange(p, src):
        for v, r in enumerate((0, T - 1)):
            remote(
                src.at[:, r], halo.at[p, row_side[v]], halo_send.at[p], halo_recv.at[p], row_dev[v]
            )
        for h in range(2):
            remote(
                colsend.at[h], halo.at[p, 3 - h], halo_send.at[p], halo_recv.at[p], col_dev[h]
            )
        for v in range(2):
            for h in range(2):
                remote(
                    corsend.at[v, h],
                    corner.at[p, row_side[v], 1 - h],
                    cor_send.at[p],
                    cor_recv.at[p],
                    cor_dev[v][h],
                )

    def reduce_stats(p, chosen, between):
        picked = jnp.where(own_frame, select(stat[...], chosen), 0.0)
        total = jnp.concatenate(
            [jnp.sum(picked[:F], axis=0, keepdims=True), jnp.sum(picked[F:], axis=0, keepdims=True)],
            axis=0,
        )
        for s, peers in enumerate(stages):
            msg[p, s] = total
            for i, dev in enumerate(peers):
                remote(msg.at[p, s], sums.at[p, s, i], ar_send.at[p, s], ar_recv.at[p, s], dev)
            if s == 0:
                between()
            n = len(peers)
            arrived(sums.at[p, s, pl.ds(0, n)], ar_recv.at[p, s])
            total = total + jnp.sum(sums[p, s, 0:n], axis=0)
        return total

    def sends_done(p):
        for s, peers in enumerate(stages):
            arrived(sums.at[p, s, pl.ds(0, len(peers))], ar_send.at[p, s])
        arrived(halo.at[p], halo_send.at[p])
        arrived(corner.at[p], cor_send.at[p])

    def coefficients(total, chosen, gain, shift):
        count = float(T * T * n_lon * n_lat * per)
        average = total[0:1] / count
        variance = total[1:2] / count - average * average
        inverse = lax.rsqrt(variance + 1e-05)
        both = jnp.concatenate(
            [jnp.broadcast_to(average, (F, 128)), jnp.broadcast_to(inverse, (F, 128))], axis=0
        )
        spread = select(jnp.where(own_frame, both, 0.0), chosen)
        coef[0:F, :] = spread[0:F]
        coef[F : 2 * F, :] = spread[F:] * (vecs[gain][None, :] * 0.5)
        coef[8:9, :] = vecs[shift][None, :] * 0.5

    def shifted(p, f, src):
        mean = coef[pl.ds(f, 1), :]
        scale = coef[pl.ds(F + f, 1), :]
        shift = coef[8:9, :]

        def act(v):
            lead = (1,) * (v.ndim - 2)
            m, k, s = (t.reshape(lead + (1, C)) for t in (mean, scale, shift))
            h = (v - m) * k + s
            return h + h * jnp.tanh(h)

        rows = jnp.concatenate([halo[p, 0, f][None], src[f], halo[p, 1, f][None]], axis=0)
        mid = act(rows.astype(F32))
        side = []
        for h in range(2):
            strip = jnp.concatenate(
                [
                    corner[p, 0, h, pl.ds(f, 1), :],
                    halo[p, 2 + h, f].astype(F32),
                    corner[p, 1, h, pl.ds(f, 1), :],
                ],
                axis=0,
            )
            side.append(act(strip)[:, None, :])
        west = jnp.concatenate([side[0], mid[:, : T - 1, :]], axis=1)
        east = jnp.concatenate([mid[:, 1:, :], side[1]], axis=1)
        taps = [v.reshape(18 * T, C) for v in (west, mid, east)]
        for b, v in enumerate(taps):
            cols[f, :, pl.ds(b * LOW, LOW)] = v[:, :LOW].astype(BF16)
        tails = [v[:, LOW:] for v in taps] + [jnp.zeros((18 * T, TAIL), F32)]
        for i in range(2):
            pair = jnp.concatenate(tails[2 * i : 2 * i + 2], axis=1)
            cols[f, :, pl.ds(3 * LOW + 128 * i, 128)] = pair.astype(BF16)

    def convolve(k, f):
        low = jnp.zeros((T * T, LOW), F32)
        for a in range(3):
            low += jnp.dot(
                cols[f, pl.ds(a * T, T * T), :], wf[k, a, :, 0:LOW], preferred_element_type=F32
            )
        side = jnp.dot(cols[f], wt[k], preferred_element_type=F32)
        tail = side[0 : T * T, 0:TAIL]
        tail = tail + side[T : T + T * T, TAIL : 2 * TAIL]
        tail = tail + side[2 * T : 2 * T + T * T, 2 * TAIL : 3 * TAIL]
        return jnp.concatenate([low, tail], axis=1)

    for f in range(F):
        x_in[f].wait()

    def first_notes(f, carry):
        note_frame(f, xv[f].astype(F32))
        return carry

    lax.fori_loop(0, F, first_notes, 0)
    to_groups = member((C, 128), 0)
    pl.semaphore_wait(barrier, len(greeted))

    def prepare():
        exchange(0, xv)
        for k in range(2):
            wf[k, :, pl.ds(3 * C, K - 3 * C), :] = jnp.zeros((3, K - 3 * C, C), BF16)
            arrived(wf.at[k, :, pl.ds(0, 3 * C)], w_sem.at[k])
            tails = [wf[k, a, :, LOW:C] for a in range(3)] + [jnp.zeros((K, TAIL), BF16)]
            for i in range(2):
                wt[k, :, pl.ds(128 * i, 128)] = jnp.concatenate(
                    tails[2 * i : 2 * i + 2], axis=1
                )
        for cp in vec_in:
            cp.wait()

    to_channels = member((128, C), 1)
    total = reduce_stats(0, to_groups, prepare)
    coefficients(total, to_channels, 0, 1)
    arrived(halo.at[0], halo_recv.at[0])
    arrived(corner.at[0], cor_recv.at[0])
    sends_done(0)

    def first_conv(f, carry):
        shifted(0, f, xv)
        acc = convolve(0, f) + (vecs[2][None, :] + emb[pl.ds(f, 1), :])
        rounded = acc.astype(BF16).reshape(T, T, C)
        hid[f] = rounded
        note_frame(f, rounded.astype(F32))
        return carry

    lax.fori_loop(0, F, first_conv, 0)

    total = reduce_stats(1, to_groups, lambda: exchange(1, hid))
    coefficients(total, to_channels, 3, 4)
    arrived(halo.at[1], halo_recv.at[1])
    arrived(corner.at[1], cor_recv.at[1])
    sends_done(1)

    def second_conv(f, carry):
        shifted(1, f, hid)
        acc = convolve(1, f) + vecs[5][None, :] + xv[f].astype(F32).reshape(T * T, C)
        o_ref[f] = acc.astype(BF16).reshape(T, T, C)
        return carry

    lax.fori_loop(0, F, second_conv, 0)


def block(n_lon, n_lat, *args):
    vm = pltpu.VMEM
    hbm = pl.BlockSpec(memory_space=pltpu.HBM)
    dma = pltpu.SemaphoreType.DMA
    n_peers = 2 * n_lat
    return pl.pallas_call(
        functools.partial(kernel, n_lon, n_lat),
        out_shape=jax.ShapeDtypeStruct((F, T, T, C), BF16),
        in_specs=[hbm] * 10,
        out_specs=pl.BlockSpec(memory_space=vm),
        scratch_shapes=[
            vm((F, T, T, C), BF16),
            vm((F, T, T, C), BF16),
            vm((2, 3, K, C), BF16),
            vm((2, K, 256), BF16),
            vm((F, 18 * T, K), BF16),
            vm((8, C), F32),
            vm((16, C), F32),
            vm((6, C), F32),
            vm((F, C), F32),
            vm((2, 2, 2, 128), F32),
            vm((2, 2, n_peers, 2, 128), F32),
            vm((2, 4, F, T, C), BF16),
            vm((2, 2, 2, 8, C), F32),
            vm((2, F, T, C), BF16),
            vm((2, 2, 8, C), F32),
            dma((F,)),
            dma((2,)),
            dma((7,)),
            dma((2, 2)),
            dma((2, 2)),
            dma((2,)),
            dma((2,)),
            dma((2,)),
            dma((2,)),
        ],
        compiler_params=pltpu.CompilerParams(collective_id=0, has_side_effects=True, vmem_limit_bytes=24 * 2**20),
    )(*[pltpu.with_memory_space_constraint(a, pltpu.HBM) for a in args])


def solution(mesh):
    n_lon, n_lat = mesh.shape["lon"], mesh.shape["lat"]
    tile = P(None, "lat", "lon", None)
    return jax.shard_map(
        functools.partial(block, n_lon, n_lat),
        mesh=mesh,
        in_specs=(tile,) + (P(),) * 9,
        out_specs=tile,
        check_vma=False,
    )
```

time: 64 us -> 46.7 us (0.73)
  local copies, waits for them, and re-layouts: 9.62 us -> 0.88 us
  Pallas kernels: 54 us -> 45.7 us
    pallas_call x1, Pallas kernels: 54 us -> 45.7 us  [block(): pl.pallas_call(functools.partial(kernel, n_lon, n_lat), out_shape=jax.Sha...]
    reshape x6 -> x0, local copies, waits for them, and re-layouts: 7.53 us -> none  [block(): row = lambda v: v.reshape(1, C)]
    unnamed x1, local copies, waits for them, and re-layouts: 2.09 us -> 0.88 us
where the time goes in v2:
time: 46.7 us; the launch traced here: 46.6 us
  Pallas kernels  45.7 us (98%)
  local copies, waits for them, and re-layouts  0.88 us (2%)
    pallas_call x1, Pallas kernels, block(): pl.pallas_call(functools.partial(kernel, n_lon, n_lat), out_shape=jax.Sha...  45.7 us

profile of v2, /device:TPU:1, one launch (start us, length us, event | category | flops | bytes accessed | tf_op | source)
XLA Modules:
  0.0 46.6 jit_solution(6518158313514262869)
XLA Ops:
  0.0 45.7 %shard_map.100 = bf16[4,16,16,320]{3,2,1,0:T(8,128)(2,1)S(1)} custom-call(bf16[4,16,16,320]{3,2,1,0:T(8,128)(2,1)} %x_hbm.1, f32[320]{0:T(512)} %g1_hbm.1, f32[320]{0:T(512)} %s1_hbm.1, bf16[3,3,320,320]{3,2,1,0:T(8,128)(2,1)} %w1_hbm.1, f32[320]{0:T(512)} %b1_hbm.1, f32[4,320]{1,0:T(4,128)} %emb_hbm.1, f32[320]{0:T(512)} %g2_hbm.1, f32[320]{0:T(512)} %s2_hbm.1, ...), custom_call_target="tpu_custom_call" | custom-call | tf_op jit(solution)/shard_map/pallas_call | solution.py:324
  45.7 0.9 %copy.12 = bf16[4,16,16,320]{3,2,1,0:T(8,128)(2,1)} copy(bf16[4,16,16,320]{3,2,1,0:T(8,128)(2,1)S(1)} %shard_map.100) | data formatting | bytes 1310720

commit v3 on v2

--- a/solution.py
+++ b/solution.py
@@ -43,7 +43,9 @@
     vecs,
     emb,
     msg,
+    msg2,
     sums,
+    sums2,
     halo,
     corner,
     colsend,
@@ -53,6 +55,8 @@
     v_sem,
     ar_send,
     ar_recv,
+    ar_send2,
+    ar_recv2,
     halo_send,
     halo_recv,
     cor_send,
@@ -124,7 +128,10 @@
         inside = (chan >= group * per) & (chan < group * per + per)
         return jnp.where(inside, 1.0, 0.0).astype(BF16)
 
-    own_frame = (lax.broadcasted_iota(jnp.int32, (8, 128), 0) & (F - 1)) == (
+    own_lanes = (lax.broadcasted_iota(jnp.int32, (8, 128), 0) & 3) == (
+        lax.broadcasted_iota(jnp.int32, (8, 128), 1) // GROUPS
+    )
+    own_low_lanes = (lax.broadcasted_iota(jnp.int32, (8, 128), 0) & 1) == (
         lax.broadcasted_iota(jnp.int32, (8, 128), 1) // GROUPS
     )
 
@@ -138,8 +145,9 @@
 
     def note_frame(f, v):
         flat = v.reshape(T * T, C)
-        stat[pl.ds(f, 1), :] = jnp.sum(flat, axis=0, keepdims=True)
-        stat[pl.ds(F + f, 1), :] = jnp.sum(flat * flat, axis=0, keepdims=True)
+        row = div(f, 2) * 4 + rem(f, 2)
+        stat[pl.ds(row, 1), :] = jnp.sum(flat, axis=0, keepdims=True)
+        stat[pl.ds(row + 2, 1), :] = jnp.sum(flat * flat, axis=0, keepdims=True)
         for h, c in enumerate((0, T - 1)):
             column = v[:, c, :]
             colsend[h, f] = column.astype(BF16)
@@ -178,45 +186,39 @@
                     cor_dev[v][h],
                 )
 
-    def reduce_stats(p, chosen, between):
-        picked = jnp.where(own_frame, select(stat[...], chosen), 0.0)
-        total = jnp.concatenate(
-            [jnp.sum(picked[:F], axis=0, keepdims=True), jnp.sum(picked[F:], axis=0, keepdims=True)],
-            axis=0,
+    def local_sums(chosen):
+        picked = jnp.where(own_lanes, select(stat[...], chosen), 0.0)
+        return jnp.concatenate(
+            [jnp.sum(picked[4 * h : 4 * h + 4], axis=0, keepdims=True) for h in range(2)], axis=0
         )
-        for s, peers in enumerate(stages):
-            msg[p, s] = total
-            for i, dev in enumerate(peers):
-                remote(msg.at[p, s], sums.at[p, s, i], ar_send.at[p, s], ar_recv.at[p, s], dev)
-            if s == 0:
-                between()
-            n = len(peers)
-            arrived(sums.at[p, s, pl.ds(0, n)], ar_recv.at[p, s])
-            total = total + jnp.sum(sums[p, s, 0:n], axis=0)
-        return total
-
-    def sends_done(p):
-        for s, peers in enumerate(stages):
-            arrived(sums.at[p, s, pl.ds(0, len(peers))], ar_send.at[p, s])
-        arrived(halo.at[p], halo_send.at[p])
-        arrived(corner.at[p], cor_send.at[p])
-
-    def coefficients(total, chosen, gain, shift):
+
+    def send_sums(s, total, out, into, send, recv):
+        out[...] = total
+        for i, dev in enumerate(stages[s]):
+            remote(out, into.at[i], send, recv, dev)
+
+    def take_sums(s, total, into, recv):
+        n = len(stages[s])
+        arrived(into.at[pl.ds(0, n)], recv)
+        return total + jnp.sum(into[0:n], axis=0)
+
+    def coefficients(h, total, chosen, gain, shift):
         count = float(T * T * n_lon * n_lat * per)
-        average = total[0:1] / count
-        variance = total[1:2] / count - average * average
-        inverse = lax.rsqrt(variance + 1e-05)
+        average = total / count
+        variance = pltpu.roll(average, 64, 1) - average * average
+        inverse = lax.rsqrt(jnp.maximum(variance, 0.0) + 1e-05)
         both = jnp.concatenate(
-            [jnp.broadcast_to(average, (F, 128)), jnp.broadcast_to(inverse, (F, 128))], axis=0
+            [jnp.broadcast_to(average, (2, 128)), jnp.broadcast_to(inverse, (2, 128))] * 2, axis=0
         )
-        spread = select(jnp.where(own_frame, both, 0.0), chosen)
-        coef[0:F, :] = spread[0:F]
-        coef[F : 2 * F, :] = spread[F:] * (vecs[gain][None, :] * 0.5)
+        spread = select(jnp.where(own_low_lanes, both, 0.0), chosen)
+        coef[4 * h : 4 * h + 2, :] = spread[0:2]
+        coef[4 * h + 2 : 4 * h + 4, :] = spread[2:4] * (vecs[gain][None, :] * 0.5)
         coef[8:9, :] = vecs[shift][None, :] * 0.5
 
     def shifted(p, f, src):
-        mean = coef[pl.ds(f, 1), :]
-        scale = coef[pl.ds(F + f, 1), :]
+        row = f // 2 * 4 + f % 2
+        mean = coef[row : row + 1, :]
+        scale = coef[row + 2 : row + 3, :]
         shift = coef[8:9, :]
 
         def act(v):
@@ -231,9 +233,9 @@
         for h in range(2):
             strip = jnp.concatenate(
                 [
-                    corner[p, 0, h, pl.ds(f, 1), :],
+                    corner[p, 0, h, f : f + 1, :],
                     halo[p, 2 + h, f].astype(F32),
-                    corner[p, 1, h, pl.ds(f, 1), :],
+                    corner[p, 1, h, f : f + 1, :],
                 ],
                 axis=0,
             )
@@ -285,35 +287,64 @@
             cp.wait()
 
     to_channels = member((128, C), 1)
-    total = reduce_stats(0, to_groups, prepare)
-    coefficients(total, to_channels, 0, 1)
+    total = local_sums(to_groups)
+    for s in range(2):
+        send_sums(s, total, msg.at[s], sums.at[s], ar_send.at[s], ar_recv.at[s])
+        if s == 0:
+            prepare()
+        total = take_sums(s, total, sums.at[s], ar_recv.at[s])
+    for h in range(2):
+        coefficients(h, total[h : h + 1], to_channels, 0, 1)
     arrived(halo.at[0], halo_recv.at[0])
     arrived(corner.at[0], cor_recv.at[0])
-    sends_done(0)
-
-    def first_conv(f, carry):
-        shifted(0, f, xv)
-        acc = convolve(0, f) + (vecs[2][None, :] + emb[pl.ds(f, 1), :])
+    for s, peers in enumerate(stages):
+        arrived(sums.at[s, pl.ds(0, len(peers))], ar_send.at[s])
+    arrived(halo.at[0], halo_send.at[0])
+    arrived(corner.at[0], cor_send.at[0])
+
+    def first_conv(f):
+        acc = convolve(0, f) + (vecs[2][None, :] + emb[f : f + 1, :])
         rounded = acc.astype(BF16).reshape(T, T, C)
         hid[f] = rounded
         note_frame(f, rounded.astype(F32))
-        return carry
-
-    lax.fori_loop(0, F, first_conv, 0)
-
-    total = reduce_stats(1, to_groups, lambda: exchange(1, hid))
-    coefficients(total, to_channels, 3, 4)
+
+    def second_conv(f):
+        acc = convolve(1, f) + vecs[5][None, :] + xv[f].astype(F32).reshape(T * T, C)
+        o_ref[f] = acc.astype(BF16).reshape(T, T, C)
+
+    totals = [None, None]
+    shifted(0, 0, xv)
+    for f in range(F):
+        if f + 1 < F:
+            shifted(0, f + 1, xv)
+        first_conv(f)
+        if f % 2 == 1:
+            h = f // 2
+            totals[h] = local_sums(to_groups)[h : h + 1]
+            send_sums(
+                0, totals[h], msg2.at[0, h], sums2.at[0, h], ar_send2.at[0, h], ar_recv2.at[0, h]
+            )
+    exchange(1, hid)
+    for h in range(2):
+        totals[h] = take_sums(0, totals[h], sums2.at[0, h], ar_recv2.at[0, h])
+        send_sums(
+            1, totals[h], msg2.at[1, h], sums2.at[1, h], ar_send2.at[1, h], ar_recv2.at[1, h]
+        )
     arrived(halo.at[1], halo_recv.at[1])
     arrived(corner.at[1], cor_recv.at[1])
-    sends_done(1)
-
-    def second_conv(f, carry):
-        shifted(1, f, hid)
-        acc = convolve(1, f) + vecs[5][None, :] + xv[f].astype(F32).reshape(T * T, C)
-        o_ref[f] = acc.astype(BF16).reshape(T, T, C)
-        return carry
-
-    lax.fori_loop(0, F, second_conv, 0)
+    for h in range(2):
+        arrived(sums2.at[0, h, pl.ds(0, len(stages[0]))], ar_send2.at[0, h])
+    arrived(halo.at[1], halo_send.at[1])
+    arrived(corner.at[1], cor_send.at[1])
+    for h in range(2):
+        totals[h] = take_sums(1, totals[h], sums2.at[1, h], ar_recv2.at[1, h])
+        coefficients(h, totals[h], to_channels, 3, 4)
+        shifted(1, 2 * h, hid)
+        shifted(1, 2 * h + 1, hid)
+        second_conv(2 * h)
+        second_conv(2 * h + 1)
+    for h in range(2):
+        arrived(sums2.at[1, h, pl.ds(0, len(stages[1]))], ar_send2.at[1, h])
 
 
 def block(n_lon, n_lat, *args):
@@ -336,8 +367,10 @@
             vm((16, C), F32),
             vm((6, C), F32),
             vm((F, C), F32),
-            vm((2, 2, 2, 128), F32),
-            vm((2, 2, n_peers, 2, 128), F32),
+            vm((2, 2, 128), F32),
+            vm((2, 2, 1, 128), F32),
+            vm((2, n_peers, 2, 128), F32),
+            vm((2, 2, n_peers, 1, 128), F32),
             vm((2, 4, F, T, C), BF16),
             vm((2, 2, 2, 8, C), F32),
             vm((2, F, T, C), BF16),
@@ -345,6 +378,8 @@
             dma((F,)),
             dma((2,)),
             dma((7,)),
+            dma((2,)),
+            dma((2,)),
             dma((2, 2)),
             dma((2, 2)),
             dma((2,)),

time: 46.7 us -> 44.1 us (0.944)
  Pallas kernels: 45.7 us -> 43.1 us
    pallas_call x1, Pallas kernels: 45.7 us -> 43.1 us  [block(): pl.pallas_call(functools.partial(kernel, n_lon, n_lat), out_shape=jax.Sha...]
where the time goes in v3:
time: 44.1 us; the launch traced here: 44 us
  Pallas kernels  43.1 us (98%)
  local copies, waits for them, and re-layouts  0.88 us (2%)
    pallas_call x1, Pallas kernels, block(): pl.pallas_call(functools.partial(kernel, n_lon, n_lat), out_shape=jax.Sha...  43.1 us
    unnamed x1, local copies, waits for them, and re-layouts  0.88 us

profile of v3, /device:TPU:1, one launch (start us, length us, event | category | flops | bytes accessed | tf_op | source)
XLA Modules:
  0.0 44.0 jit_solution(2245230961048898154)
XLA Ops:
  0.0 43.1 %shard_map.100 = bf16[4,16,16,320]{3,2,1,0:T(8,128)(2,1)S(1)} custom-call(bf16[4,16,16,320]{3,2,1,0:T(8,128)(2,1)} %x_hbm.1, f32[320]{0:T(512)} %g1_hbm.1, f32[320]{0:T(512)} %s1_hbm.1, bf16[3,3,320,320]{3,2,1,0:T(8,128)(2,1)} %w1_hbm.1, f32[320]{0:T(512)} %b1_hbm.1, f32[4,320]{1,0:T(4,128)} %emb_hbm.1, f32[320]{0:T(512)} %g2_hbm.1, f32[320]{0:T(512)} %s2_hbm.1, ...), custom_call_target="tpu_custom_call" | custom-call | tf_op jit(solution)/shard_map/pallas_call | solution.py:355
  43.1 0.9 %copy.12 = bf16[4,16,16,320]{3,2,1,0:T(8,128)(2,1)} copy(bf16[4,16,16,320]{3,2,1,0:T(8,128)(2,1)S(1)} %shard_map.100) | data formatting | bytes 1310720

commit v4 on v3

--- a/solution.py
+++ b/solution.py
@@ -37,7 +37,11 @@
     hid,
     wf,
     wt,
+    raw,
     cols,
+    to_groups,
+    to_lanes,
+    wide,
     stat,
     coef,
     vecs,
@@ -75,11 +79,15 @@
     def flip(bit, on):
         return 1 - bit if on else bit
 
+    def hops(step, n):
+        return min(step, n - step)
+
+    x_hops = (0, 2, 1, 1)
     stages = [[], []]
-    for d in range(1, 2 * n_y):
+    for d in sorted(range(1, 2 * n_y), key=lambda d: -hops(d // 2, n_y)):
         to_y = rem(y + d // 2, n_y)
         stages[0].append((to_y * 4 + x_hi * 2 + flip(core, d % 2), lat))
-    for d in range(1, 4 * n_z):
+    for d in sorted(range(1, 4 * n_z), key=lambda d: -hops(d // 4, n_z) - x_hops[d % 4]):
         to_z = rem(z + d // 4, n_z)
         to_lon = y * 4 + flip(x_hi, d & 1) * 2 + core
         stages[1].append((to_lon, flip(x_lo, d & 2) * n_z + to_z))
@@ -96,8 +104,7 @@
     ]
 
     barrier = pltpu.get_barrier_semaphore()
-    greeted = [dev for stage in stages for dev in stage]
-    greeted += row_dev + col_dev + cor_dev[0] + cor_dev[1]
+    greeted = stages[1] + stages[0] + cor_dev[0] + cor_dev[1] + row_dev + col_dev
     for dev in greeted:
         pl.semaphore_signal(barrier, inc=1, device_id=dev, device_id_type=MESH)
 
@@ -122,11 +129,12 @@
 
     per = C // GROUPS
 
-    def member(shape, channel_dim):
-        chan = lax.broadcasted_iota(jnp.int32, shape, channel_dim)
-        group = lax.broadcasted_iota(jnp.int32, shape, 1 - channel_dim) & (GROUPS - 1)
+    def member(chan, group):
         inside = (chan >= group * per) & (chan < group * per + per)
         return jnp.where(inside, 1.0, 0.0).astype(BF16)
+
+    def iota(shape, dim):
+        return lax.broadcasted_iota(jnp.int32, shape, dim)
 
     own_lanes = (lax.broadcasted_iota(jnp.int32, (8, 128), 0) & 3) == (
         lax.broadcasted_iota(jnp.int32, (8, 128), 1) // GROUPS
@@ -148,6 +156,8 @@
         row = div(f, 2) * 4 + rem(f, 2)
         stat[pl.ds(row, 1), :] = jnp.sum(flat, axis=0, keepdims=True)
         stat[pl.ds(row + 2, 1), :] = jnp.sum(flat * flat, axis=0, keepdims=True)
+
+    def note_edges(f, v):
         for h, c in enumerate((0, T - 1)):
             column = v[:, c, :]
             colsend[h, f] = column.astype(BF16)
@@ -172,10 +182,12 @@
             remote(
                 src.at[:, r], halo.at[p, row_side[v]], halo_send.at[p], halo_recv.at[p], row_dev[v]
             )
-        for h in range(2):
-            remote(
-                colsend.at[h], halo.at[p, 3 - h], halo_send.at[p], halo_recv.at[p], col_dev[h]
-            )
+
+        def edges(f, carry):
+            note_edges(f, src[f].astype(F32))
+            return carry
+
+        lax.fori_loop(0, F, edges, 0)
         for v in range(2):
             for h in range(2):
                 remote(
@@ -185,9 +197,11 @@
                     cor_recv.at[p],
                     cor_dev[v][h],
                 )
-
-    def local_sums(chosen):
-        picked = jnp.where(own_lanes, select(stat[...], chosen), 0.0)
+        for h in range(2):
+            remote(colsend.at[h], halo.at[p, 3 - h], halo_send.at[p], halo_recv.at[p], col_dev[h])
+
+    def local_sums():
+        picked = jnp.where(own_lanes, select(stat[...], to_groups[...]), 0.0)
         return jnp.concatenate(
             [jnp.sum(picked[4 * h : 4 * h + 4], axis=0, keepdims=True) for h in range(2)], axis=0
         )
@@ -202,7 +216,7 @@
         arrived(into.at[pl.ds(0, n)], recv)
         return total + jnp.sum(into[0:n], axis=0)
 
-    def coefficients(h, total, chosen, gain, shift):
+    def coefficients(p, h, total):
         count = float(T * T * n_lon * n_lat * per)
         average = total / count
         variance = pltpu.roll(average, 64, 1) - average * average
@@ -210,45 +224,51 @@
         both = jnp.concatenate(
             [jnp.broadcast_to(average, (2, 128)), jnp.broadcast_to(inverse, (2, 128))] * 2, axis=0
         )
-        spread = select(jnp.where(own_low_lanes, both, 0.0), chosen)
+        spread = select(jnp.where(own_low_lanes, both, 0.0), to_lanes[...])
         coef[4 * h : 4 * h + 2, :] = spread[0:2]
-        coef[4 * h + 2 : 4 * h + 4, :] = spread[2:4] * (vecs[gain][None, :] * 0.5)
-        coef[8:9, :] = vecs[shift][None, :] * 0.5
-
-    def shifted(p, f, src):
+        coef[4 * h + 2 : 4 * h + 4, :] = spread[2:4] * wide[2 * p : 2 * p + 1, :]
+
+    def widen(v):
+        return jnp.concatenate(
+            [v[:, :LOW]] * 3 + [v[:, LOW:]] * 3 + [jnp.zeros((1, K - 3 * C), F32)], axis=1
+        )
+
+    def arrange(p, src):
+        def one(f, carry):
+            rows = jnp.concatenate([halo[p, 0, f][None], src[f], halo[p, 1, f][None]], axis=0)
+            mid = rows.astype(F32)
+            side = []
+            for h in range(2):
+                strip = jnp.concatenate(
+                    [
+                        corner[p, 0, h, pl.ds(f, 1), :],
+                        halo[p, 2 + h, f].astype(F32),
+                        corner[p, 1, h, pl.ds(f, 1), :],
+                    ],
+                    axis=0,
+                )
+                side.append(strip[:, None, :])
+            west = jnp.concatenate([side[0], mid[:, : T - 1, :]], axis=1)
+            east = jnp.concatenate([mid[:, 1:, :], side[1]], axis=1)
+            taps = [v.reshape(18 * T, C) for v in (west, mid, east)]
+            for b, v in enumerate(taps):
+                raw[f, :, pl.ds(b * LOW, LOW)] = v[:, :LOW].astype(BF16)
+            tails = [v[:, LOW:] for v in taps] + [jnp.zeros((18 * T, TAIL), F32)]
+            for i in range(2):
+                pair = jnp.concatenate(tails[2 * i : 2 * i + 2], axis=1)
+                raw[f, :, pl.ds(3 * LOW + 128 * i, 128)] = pair.astype(BF16)
+            return carry
+
+        lax.fori_loop(0, F, one, 0)
+
+    def activate(p, f):
         row = f // 2 * 4 + f % 2
-        mean = coef[row : row + 1, :]
-        scale = coef[row + 2 : row + 3, :]
-        shift = coef[8:9, :]
-
-        def act(v):
-            lead = (1,) * (v.ndim - 2)
-            m, k, s = (t.reshape(lead + (1, C)) for t in (mean, scale, shift))
-            h = (v - m) * k + s
-            return h + h * jnp.tanh(h)
-
-        rows = jnp.concatenate([halo[p, 0, f][None], src[f], halo[p, 1, f][None]], axis=0)
-        mid = act(rows.astype(F32))
-        side = []
-        for h in range(2):
-            strip = jnp.concatenate(
-                [
-                    corner[p, 0, h, f : f + 1, :],
-                    halo[p, 2 + h, f].astype(F32),
-                    corner[p, 1, h, f : f + 1, :],
-                ],
-                axis=0,
-            )
-            side.append(act(strip)[:, None, :])
-        west = jnp.concatenate([side[0], mid[:, : T - 1, :]], axis=1)
-        east = jnp.concatenate([mid[:, 1:, :], side[1]], axis=1)
-        taps = [v.reshape(18 * T, C) for v in (west, mid, east)]
-        for b, v in enumerate(taps):
-            cols[f, :, pl.ds(b * LOW, LOW)] = v[:, :LOW].astype(BF16)
-        tails = [v[:, LOW:] for v in taps] + [jnp.zeros((18 * T, TAIL), F32)]
-        for i in range(2):
-            pair = jnp.concatenate(tails[2 * i : 2 * i + 2], axis=1)
-            cols[f, :, pl.ds(3 * LOW + 128 * i, 128)] = pair.astype(BF16)
+        for i in range(K // LOW):
+            lanes = pl.ds(i * LOW, LOW)
+            v = raw[f, :, lanes].astype(F32)
+            h = (v - coef[row : row + 1, lanes]) * coef[row + 2 : row + 3, lanes]
+            h = h + wide[2 * p + 1 : 2 * p + 2, lanes]
+            cols[f, :, lanes] = (h + h * jnp.tanh(h)).astype(BF16)
 
     def convolve(k, f):
         low = jnp.zeros((T * T, LOW), F32)
@@ -270,11 +290,15 @@
         return carry
 
     lax.fori_loop(0, F, first_notes, 0)
-    to_groups = member((C, 128), 0)
+    to_groups[...] = member(iota((C, 128), 0), iota((C, 128), 1) & (GROUPS - 1))
     pl.semaphore_wait(barrier, len(greeted))
 
     def prepare():
         exchange(0, xv)
+        lane = iota((128, K), 1)
+        chan = jnp.where(lane < 3 * LOW, lane & (LOW - 1), LOW + (lane & (TAIL - 1)))
+        chan = jnp.where(lane < 3 * C, chan, -1)
+        to_lanes[...] = member(chan, iota((128, K), 0) & (GROUPS - 1))
         for k in range(2):
             wf[k, :, pl.ds(3 * C, K - 3 * C), :] = jnp.zeros((3, K - 3 * C, C), BF16)
             arrived(wf.at[k, :, pl.ds(0, 3 * C)], w_sem.at[k])
@@ -285,42 +309,39 @@
                 )
         for cp in vec_in:
             cp.wait()
-
-    to_channels = member((128, C), 1)
-    total = local_sums(to_groups)
+        for row, i in enumerate((0, 1, 3, 4)):
+            wide[row : row + 1, :] = widen(vecs[i : i + 1, :] * 0.5)
+
+    total = local_sums()
     for s in range(2):
         send_sums(s, total, msg.at[s], sums.at[s], ar_send.at[s], ar_recv.at[s])
         if s == 0:
             prepare()
+        else:
+            arrived(halo.at[0], halo_recv.at[0])
+            arrived(corner.at[0], cor_recv.at[0])
+            arrange(0, xv)
         total = take_sums(s, total, sums.at[s], ar_recv.at[s])
     for h in range(2):
-        coefficients(h, total[h : h + 1], to_channels, 0, 1)
-    arrived(halo.at[0], halo_recv.at[0])
-    arrived(corner.at[0], cor_recv.at[0])
+        coefficients(0, h, total[h : h + 1])
     for s, peers in enumerate(stages):
         arrived(sums.at[s, pl.ds(0, len(peers))], ar_send.at[s])
     arrived(halo.at[0], halo_send.at[0])
     arrived(corner.at[0], cor_send.at[0])
 
-    def first_conv(f):
-        acc = convolve(0, f) + (vecs[2][None, :] + emb[f : f + 1, :])
+    totals = [None, None]
+    activate(0, 0)
+    for f in range(F):
+        acc = convolve(0, f)
+        if f + 1 < F:
+            activate(0, f + 1)
+        acc = acc + (vecs[2:3, :] + emb[f : f + 1, :])
         rounded = acc.astype(BF16).reshape(T, T, C)
         hid[f] = rounded
         note_frame(f, rounded.astype(F32))
-
-    def second_conv(f):
-        acc = convolve(1, f) + vecs[5][None, :] + xv[f].astype(F32).reshape(T * T, C)
-        o_ref[f] = acc.astype(BF16).reshape(T, T, C)
-
-    totals = [None, None]
-    shifted(0, 0, xv)
-    for f in range(F):
-        if f + 1 < F:
-            shifted(0, f + 1, xv)
-        first_conv(f)
         if f % 2 == 1:
             h = f // 2
-            totals[h] = local_sums(to_groups)[h : h + 1]
+            totals[h] = local_sums()[h : h + 1]
             send_sums(
                 0, totals[h], msg2.at[0, h], sums2.at[0, h], ar_send2.at[0, h], ar_recv2.at[0, h]
             )
@@ -332,17 +353,22 @@
         )
     arrived(halo.at[1], halo_recv.at[1])
     arrived(corner.at[1], cor_recv.at[1])
+    arrange(1, hid)
     for h in range(2):
         arrived(sums2.at[0, h, pl.ds(0, len(stages[0]))], ar_send2.at[0, h])
     arrived(halo.at[1], halo_send.at[1])
     arrived(corner.at[1], cor_send.at[1])
+
     for h in range(2):
         totals[h] = take_sums(1, totals[h], sums2.at[1, h], ar_recv2.at[1, h])
-        coefficients(h, totals[h], to_channels, 3, 4)
-        shifted(1, 2 * h, hid)
-        shifted(1, 2 * h + 1, hid)
-        second_conv(2 * h)
-        second_conv(2 * h + 1)
+        coefficients(1, h, totals[h])
+        activate(1, 2 * h)
+        for f in (2 * h, 2 * h + 1):
+            acc = convolve(1, f)
+            if f == 2 * h:
+                activate(1, f + 1)
+            acc = acc + vecs[5:6, :] + xv[f].astype(F32).reshape(T * T, C)
+            o_ref[f] = acc.astype(BF16).reshape(T, T, C)
     for h in range(2):
         arrived(sums2.at[1, h, pl.ds(0, len(stages[1]))], ar_send2.at[1, h])
 
@@ -363,8 +389,12 @@
             vm((2, 3, K, C), BF16),
             vm((2, K, 256), BF16),
             vm((F, 18 * T, K), BF16),
+            vm((F, 18 * T, K), BF16),
+            vm((C, 128), BF16),
+            vm((128, K), BF16),
+            vm((4, K), F32),
             vm((8, C), F32),
-            vm((16, C), F32),
+            vm((8, K), F32),
             vm((6, C), F32),
             vm((F, C), F32),
             vm((2, 2, 128), F32),
@@ -372,9 +402,9 @@
             vm((2, n_peers, 2, 128), F32),
             vm((2, 2, n_peers, 1, 128), F32),
             vm((2, 4, F, T, C), BF16),
-            vm((2, 2, 2, 8, C), F32),
+            vm((2, 2, 2, F, C), F32),
             vm((2, F, T, C), BF16),
-            vm((2, 2, 8, C), F32),
+            vm((2, 2, F, C), F32),
             dma((F,)),
             dma((2,)),
             dma((7,)),

time: 44.1 us -> 42.9 us (0.973)
  Pallas kernels: 43.1 us -> 41.9 us
    pallas_call x1, Pallas kernels: 43.1 us -> 41.9 us  [block(): pl.pallas_call(functools.partial(kernel, n_lon, n_lat), out_shape=jax.Sha...]
where the time goes in v4:
time: 42.9 us; the launch traced here: 42.7 us
  Pallas kernels  41.9 us (98%)
  local copies, waits for them, and re-layouts  0.88 us (2%)
    pallas_call x1, Pallas kernels, block(): pl.pallas_call(functools.partial(kernel, n_lon, n_lat), out_shape=jax.Sha...  41.9 us
    unnamed x1, local copies, waits for them, and re-layouts  0.88 us

profile of v4, /device:TPU:1, one launch (start us, length us, event | category | flops | bytes accessed | tf_op | source)
XLA Modules:
  0.0 42.7 jit_solution(6546822392803338953)
XLA Ops:
  0.0 41.9 %shard_map.100 = bf16[4,16,16,320]{3,2,1,0:T(8,128)(2,1)S(1)} custom-call(bf16[4,16,16,320]{3,2,1,0:T(8,128)(2,1)} %x_hbm.1, f32[320]{0:T(512)} %g1_hbm.1, f32[320]{0:T(512)} %s1_hbm.1, bf16[3,3,320,320]{3,2,1,0:T(8,128)(2,1)} %w1_hbm.1, f32[320]{0:T(512)} %b1_hbm.1, f32[4,320]{1,0:T(4,128)} %emb_hbm.1, f32[320]{0:T(512)} %g2_hbm.1, f32[320]{0:T(512)} %s2_hbm.1, ...), custom_call_target="tpu_custom_call" | custom-call | tf_op jit(solution)/shard_map/pallas_call | solution.py:381
  41.9 0.9 %copy.12 = bf16[4,16,16,320]{3,2,1,0:T(8,128)(2,1)} copy(bf16[4,16,16,320]{3,2,1,0:T(8,128)(2,1)S(1)} %shard_map.100) | data formatting | bytes 1310720

commit v5 on v4

--- a/solution.py
+++ b/solution.py
@@ -72,10 +72,6 @@
     y, x_hi, core = div(lon, 4), rem(div(lon, 2), 2), rem(lon, 2)
     x_lo, z = div(lat, n_z), rem(lat, n_z)
 
-    x_in = [pltpu.make_async_copy(x_hbm.at[f], xv.at[f], x_sem.at[f]) for f in range(F)]
-    for cp in x_in:
-        cp.start()
-
     def flip(bit, on):
         return 1 - bit if on else bit
 
@@ -103,16 +99,18 @@
         for v in range(2)
     ]
 
+    greeted = stages[1] + stages[0] + cor_dev[0] + cor_dev[1] + row_dev + col_dev
     barrier = pltpu.get_barrier_semaphore()
-    greeted = stages[1] + stages[0] + cor_dev[0] + cor_dev[1] + row_dev + col_dev
     for dev in greeted:
         pl.semaphore_signal(barrier, inc=1, device_id=dev, device_id_type=MESH)
+    for f in range(F):
+        pltpu.make_async_copy(x_hbm.at[f], xv.at[f], x_sem).start()
 
     vec_in = [
-        pltpu.make_async_copy(hbm, vecs.at[i], v_sem.at[i])
+        pltpu.make_async_copy(hbm, vecs.at[i, 0], v_sem.at[0])
         for i, hbm in enumerate((g1_hbm, s1_hbm, b1_hbm, g2_hbm, s2_hbm, b2_hbm))
     ]
-    vec_in.append(pltpu.make_async_copy(emb_hbm, emb, v_sem.at[6]))
+    vec_in.append(pltpu.make_async_copy(emb_hbm, emb, v_sem.at[1]))
     for cp in vec_in:
         cp.start()
     for k, hbm in enumerate((w1_hbm, w2_hbm)):
@@ -180,7 +178,7 @@
     def exchange(p, src):
         for v, r in enumerate((0, T - 1)):
             remote(
-                src.at[:, r], halo.at[p, row_side[v]], halo_send.at[p], halo_recv.at[p], row_dev[v]
+                src.at[:, r], halo.at[p, row_side[v]], halo_send, halo_recv.at[p], row_dev[v]
             )
 
         def edges(f, carry):
@@ -193,12 +191,12 @@
                 remote(
                     corsend.at[v, h],
                     corner.at[p, row_side[v], 1 - h],
-                    cor_send.at[p],
+                    cor_send,
                     cor_recv.at[p],
                     cor_dev[v][h],
                 )
         for h in range(2):
-            remote(colsend.at[h], halo.at[p, 3 - h], halo_send.at[p], halo_recv.at[p], col_dev[h])
+            remote(colsend.at[h], halo.at[p, 3 - h], halo_send, halo_recv.at[p], col_dev[h])
 
     def local_sums():
         picked = jnp.where(own_lanes, select(stat[...], to_groups[...]), 0.0)
@@ -206,15 +204,18 @@
             [jnp.sum(picked[4 * h : 4 * h + 4], axis=0, keepdims=True) for h in range(2)], axis=0
         )
 
+    def slots(s, h, n_halves):
+        n = [len(stage) for stage in stages]
+        return pl.ds(n[0] * h if s == 0 else n[0] * n_halves + n[1] * h, n[s])
+
     def send_sums(s, total, out, into, send, recv):
         out[...] = total
         for i, dev in enumerate(stages[s]):
             remote(out, into.at[i], send, recv, dev)
 
-    def take_sums(s, total, into, recv):
-        n = len(stages[s])
-        arrived(into.at[pl.ds(0, n)], recv)
-        return total + jnp.sum(into[0:n], axis=0)
+    def take_sums(total, into, recv):
+        arrived(into, recv)
+        return total + jnp.sum(into[...], axis=0)
 
     def coefficients(p, h, total):
         count = float(T * T * n_lon * n_lat * per)
@@ -225,8 +226,9 @@
             [jnp.broadcast_to(average, (2, 128)), jnp.broadcast_to(inverse, (2, 128))] * 2, axis=0
         )
         spread = select(jnp.where(own_low_lanes, both, 0.0), to_lanes[...])
-        coef[4 * h : 4 * h + 2, :] = spread[0:2]
-        coef[4 * h + 2 : 4 * h + 4, :] = spread[2:4] * wide[2 * p : 2 * p + 1, :]
+        scale = spread[2:4] * wide[2 * p : 2 * p + 1, :]
+        coef[4 * h : 4 * h + 2, :] = wide[2 * p + 1 : 2 * p + 2, :] - spread[0:2] * scale
+        coef[4 * h + 2 : 4 * h + 4, :] = scale
 
     def widen(v):
         return jnp.concatenate(
@@ -261,13 +263,12 @@
 
         lax.fori_loop(0, F, one, 0)
 
-    def activate(p, f):
+    def activate(f):
         row = f // 2 * 4 + f % 2
         for i in range(K // LOW):
             lanes = pl.ds(i * LOW, LOW)
             v = raw[f, :, lanes].astype(F32)
-            h = (v - coef[row : row + 1, lanes]) * coef[row + 2 : row + 3, lanes]
-            h = h + wide[2 * p + 1 : 2 * p + 2, lanes]
+            h = v * coef[row + 2 : row + 3, lanes] + coef[row : row + 1, lanes]
             cols[f, :, lanes] = (h + h * jnp.tanh(h)).astype(BF16)
 
     def convolve(k, f):
@@ -282,8 +283,7 @@
         tail = tail + side[2 * T : 2 * T + T * T, 2 * TAIL : 3 * TAIL]
         return jnp.concatenate([low, tail], axis=1)
 
-    for f in range(F):
-        x_in[f].wait()
+    arrived(xv, x_sem)
 
     def first_notes(f, carry):
         note_frame(f, xv[f].astype(F32))
@@ -291,6 +291,7 @@
 
     lax.fori_loop(0, F, first_notes, 0)
     to_groups[...] = member(iota((C, 128), 0), iota((C, 128), 1) & (GROUPS - 1))
+    total = local_sums()
     pl.semaphore_wait(barrier, len(greeted))
 
     def prepare():
@@ -307,77 +308,71 @@
                 wt[k, :, pl.ds(128 * i, 128)] = jnp.concatenate(
                     tails[2 * i : 2 * i + 2], axis=1
                 )
-        for cp in vec_in:
-            cp.wait()
+        arrived(vecs, v_sem.at[0])
+        arrived(emb, v_sem.at[1])
         for row, i in enumerate((0, 1, 3, 4)):
-            wide[row : row + 1, :] = widen(vecs[i : i + 1, :] * 0.5)
-
-    total = local_sums()
+            wide[row : row + 1, :] = widen(vecs[i] * 0.5)
+
     for s in range(2):
-        send_sums(s, total, msg.at[s], sums.at[s], ar_send.at[s], ar_recv.at[s])
+        into = sums.at[slots(s, 0, 1)]
+        send_sums(s, total, msg.at[s], into, ar_send, ar_recv.at[s])
         if s == 0:
             prepare()
         else:
             arrived(halo.at[0], halo_recv.at[0])
             arrived(corner.at[0], cor_recv.at[0])
             arrange(0, xv)
-        total = take_sums(s, total, sums.at[s], ar_recv.at[s])
+        total = take_sums(total, into, ar_recv.at[s])
     for h in range(2):
         coefficients(0, h, total[h : h + 1])
-    for s, peers in enumerate(stages):
-        arrived(sums.at[s, pl.ds(0, len(peers))], ar_send.at[s])
-    arrived(halo.at[0], halo_send.at[0])
-    arrived(corner.at[0], cor_send.at[0])
+    arrived(sums, ar_send)
+    arrived(halo.at[0], halo_send)
+    arrived(corner.at[0], cor_send)
 
     totals = [None, None]
-    activate(0, 0)
+    activate(0)
     for f in range(F):
         acc = convolve(0, f)
         if f + 1 < F:
-            activate(0, f + 1)
-        acc = acc + (vecs[2:3, :] + emb[f : f + 1, :])
+            activate(f + 1)
+        acc = acc + (vecs[2] + emb[f : f + 1, :])
         rounded = acc.astype(BF16).reshape(T, T, C)
         hid[f] = rounded
         note_frame(f, rounded.astype(F32))
         if f % 2 == 1:
             h = f // 2
             totals[h] = local_sums()[h : h + 1]
-            send_sums(
-                0, totals[h], msg2.at[0, h], sums2.at[0, h], ar_send2.at[0, h], ar_recv2.at[0, h]
-            )
+            into = sums2.at[slots(0, h, 2)]
+            send_sums(0, totals[h], msg2.at[0, h], into, ar_send2, ar_recv2.at[0, h])
     exchange(1, hid)
     for h in range(2):
-        totals[h] = take_sums(0, totals[h], sums2.at[0, h], ar_recv2.at[0, h])
-        send_sums(
-            1, totals[h], msg2.at[1, h], sums2.at[1, h], ar_send2.at[1, h], ar_recv2.at[1, h]
-        )
+        totals[h] = take_sums(totals[h], sums2.at[slots(0, h, 2)], ar_recv2.at[0, h])
+        into = sums2.at[slots(1, h, 2)]
+        send_sums(1, totals[h], msg2.at[1, h], into, ar_send2, ar_recv2.at[1, h])
     arrived(halo.at[1], halo_recv.at[1])
     arrived(corner.at[1], cor_recv.at[1])
     arrange(1, hid)
+    arrived(halo.at[1], halo_send)
+    arrived(corner.at[1], cor_send)
+
     for h in range(2):
-        arrived(sums2.at[0, h, pl.ds(0, len(stages[0]))], ar_send2.at[0, h])
-    arrived(halo.at[1], halo_send.at[1])
-    arrived(corner.at[1], cor_send.at[1])
-
-    for h in range(2):
-        totals[h] = take_sums(1, totals[h], sums2.at[1, h], ar_recv2.at[1, h])
+        totals[h] = take_sums(totals[h], sums2.at[slots(1, h, 2)], ar_recv2.at[1, h])
         coefficients(1, h, totals[h])
-        activate(1, 2 * h)
+        activate(2 * h)
         for f in (2 * h, 2 * h + 1):
             acc = convolve(1, f)
             if f == 2 * h:
-                activate(1, f + 1)
-            acc = acc + vecs[5:6, :] + xv[f].astype(F32).reshape(T * T, C)
+                activate(f + 1)
+            acc = acc + vecs[5] + xv[f].astype(F32).reshape(T * T, C)
             o_ref[f] = acc.astype(BF16).reshape(T, T, C)
-    for h in range(2):
-        arrived(sums2.at[1, h, pl.ds(0, len(stages[1]))], ar_send2.at[1, h])
+    arrived(sums2, ar_send2)
 
 
 def block(n_lon, n_lat, *args):
     vm = pltpu.VMEM
     hbm = pl.BlockSpec(memory_space=pltpu.HBM)
     dma = pltpu.SemaphoreType.DMA
-    n_peers = 2 * n_lat
+    n_peers = n_lon // 2 - 1 + 2 * n_lat - 1
     return pl.pallas_call(
         functools.partial(kernel, n_lon, n_lat),
         out_shape=jax.ShapeDtypeStruct((F, T, T, C), BF16),
@@ -395,26 +390,26 @@
             vm((4, K), F32),
             vm((8, C), F32),
             vm((8, K), F32),
-            vm((6, C), F32),
+            vm((6, 1, C), F32),
             vm((F, C), F32),
             vm((2, 2, 128), F32),
             vm((2, 2, 1, 128), F32),
-            vm((2, n_peers, 2, 128), F32),
-            vm((2, 2, n_peers, 1, 128), F32),
+            vm((n_peers, 2, 128), F32),
+            vm((2 * n_peers, 1, 128), F32),
             vm((2, 4, F, T, C), BF16),
             vm((2, 2, 2, F, C), F32),
             vm((2, F, T, C), BF16),
             vm((2, 2, F, C), F32),
-            dma((F,)),
-            dma((2,)),
-            dma((7,)),
+            dma,
             dma((2,)),
             dma((2,)),
+            dma,
+            dma((2,)),
+            dma,
             dma((2, 2)),
-            dma((2, 2)),
+            dma,
             dma((2,)),
-            dma((2,)),
-            dma((2,)),
+            dma,
             dma((2,)),
         ],
         compiler_params=pltpu.CompilerParams(collective_id=0, has_side_effects=True, vmem_limit_bytes=24 * 2**20),

time: 42.9 us -> 42.4 us (0.988)
  Pallas kernels: 41.9 us -> 41.4 us
where the time goes in v5:
time: 42.4 us; the launch traced here: 42.3 us
  Pallas kernels  41.4 us (98%)
  local copies, waits for them, and re-layouts  0.88 us (2%)
    pallas_call x1, Pallas kernels, block(): pl.pallas_call(functools.partial(kernel, n_lon, n_lat), out_shape=jax.Sha...  41.4 us
    unnamed x1, local copies, waits for them, and re-layouts  0.88 us

profile of v5, /device:TPU:1, one launch (start us, length us, event | category | flops | bytes accessed | tf_op | source)
XLA Modules:
  0.0 42.3 jit_solution(1463301736327395148)
XLA Ops:
  0.0 41.4 %shard_map.100 = bf16[4,16,16,320]{3,2,1,0:T(8,128)(2,1)S(1)} custom-call(bf16[4,16,16,320]{3,2,1,0:T(8,128)(2,1)} %x_hbm.1, f32[320]{0:T(512)} %g1_hbm.1, f32[320]{0:T(512)} %s1_hbm.1, bf16[3,3,320,320]{3,2,1,0:T(8,128)(2,1)} %w1_hbm.1, f32[320]{0:T(512)} %b1_hbm.1, f32[4,320]{1,0:T(4,128)} %emb_hbm.1, f32[320]{0:T(512)} %g2_hbm.1, f32[320]{0:T(512)} %s2_hbm.1, ...), custom_call_target="tpu_custom_call" | custom-call | tf_op jit(solution)/shard_map/pallas_call | solution.py:376
  41.4 0.9 %copy.12 = bf16[4,16,16,320]{3,2,1,0:T(8,128)(2,1)} copy(bf16[4,16,16,320]{3,2,1,0:T(8,128)(2,1)S(1)} %shard_map.100) | data formatting | bytes 1310720

commit v6 on v5

--- a/solution.py
+++ b/solution.py
@@ -330,10 +330,11 @@
     arrived(corner.at[0], cor_send)
 
     totals = [None, None]
-    activate(0)
     for f in range(F):
+        if f % 2 == 0:
+            activate(f)
         acc = convolve(0, f)
-        if f + 1 < F:
+        if f % 2 == 0:
             activate(f + 1)
         acc = acc + (vecs[2] + emb[f : f + 1, :])
         rounded = acc.astype(BF16).reshape(T, T, C)

time: 42.4 us -> 42.1 us (level)
  no operation moved by 1% of the time
where the time goes in v6:
time: 42.1 us; the launch traced here: 42 us
  Pallas kernels  41.1 us (98%)
  local copies, waits for them, and re-layouts  0.88 us (2%)
    pallas_call x1, Pallas kernels, block(): pl.pallas_call(functools.partial(kernel, n_lon, n_lat), out_shape=jax.Sha...  41.1 us
    unnamed x1, local copies, waits for them, and re-layouts  0.88 us

profile of v6, /device:TPU:1, one launch (start us, length us, event | category | flops | bytes accessed | tf_op | source)
XLA Modules:
  0.0 42.0 jit_solution(13425103541392730128)
XLA Ops:
  0.0 41.1 %shard_map.100 = bf16[4,16,16,320]{3,2,1,0:T(8,128)(2,1)S(1)} custom-call(bf16[4,16,16,320]{3,2,1,0:T(8,128)(2,1)} %x_hbm.1, f32[320]{0:T(512)} %g1_hbm.1, f32[320]{0:T(512)} %s1_hbm.1, bf16[3,3,320,320]{3,2,1,0:T(8,128)(2,1)} %w1_hbm.1, f32[320]{0:T(512)} %b1_hbm.1, f32[4,320]{1,0:T(4,128)} %emb_hbm.1, f32[320]{0:T(512)} %g2_hbm.1, f32[320]{0:T(512)} %s2_hbm.1, ...), custom_call_target="tpu_custom_call" | custom-call | tf_op jit(solution)/shard_map/pallas_call | solution.py:377
  41.1 0.9 %copy.12 = bf16[4,16,16,320]{3,2,1,0:T(8,128)(2,1)} copy(bf16[4,16,16,320]{3,2,1,0:T(8,128)(2,1)S(1)} %shard_map.100) | data formatting | bytes 1310720
